TPU v7x, 32 devices: a whole 2x2x4 slice. The times are simulated.
32 devices in a mesh: section: 2 (over x), dp: 16 (over z, y, core).
Axes of the slice: x: 2, y: 2, z: 4, core: 2. Of those that a mesh axis runs over, the one named last changes fastest.
Arguments:
- inputs: bfloat16 [2048, 8192], P('dp', 'section'), may hold values from -6 to 6
- cotangent: bfloat16 [2048, 8192], P('dp', 'section'), may hold values from -6 to 6
- weights: bfloat16 [2, 64, 8192], P('section'), may hold values from -0.0625 to 0.0625
- momentum: bfloat16 [2, 16, 64, 8192], P('section', 'dp'), may hold values from -6 to 6
- keep_index: int32 [2, 16, 128, 32], P('section', 'dp'), may hold values from 0 to 4095, as said below
Outputs:
- momentum_out: bfloat16 [2, 16, 64, 8192], P('section', 'dp')
- update: bfloat16 [2, 16, 64, 8192], P('section', 'dp')
Inputs may be any that keep to these rules, and one draw needn't show every extreme that they name: `keep_index`: the 32 positions of one block of one replica and layer are all different.
All inputs are finite; a program needn't handle non-finite values.
Results may differ from a plain program's by a relative error of at most 0.0095.
Values may be sent and summed in bfloat16 or wider, within the bound.
A program may use at most 64 MiB of HBM per device.

v0:
```python
import math

import jax
import jax.numpy as jnp
from jax import lax
from jax.sharding import PartitionSpec as P

MICRO = 8


DECAY = 0.999


def from_behind(value, axis, steps):
    count = lax.axis_size(axis)
    leading, last = (max(0, -steps), min(count, count - steps))
    return lax.ppermute(value, axis, [(source, source + steps) for source in range(leading, last)])


def dct_basis(length):
    freq = jnp.arange(length, dtype=jnp.float32)[:, None]
    position = jnp.arange(length, dtype=jnp.float32)[None, :]
    dct_table = jnp.cos(math.pi * (position + 0.5) * freq / length) * math.sqrt(2.0 / length)
    return jnp.where(freq == 0, dct_table * math.sqrt(0.5), dct_table)


def forward_groups(field_in, dct_table):
    row_count, columns = field_in.shape
    blocks = field_in.reshape(row_count // 64, 64, columns // 64, 64)
    coeffs = jnp.einsum(
        "kn,anbm,jm->akbj", dct_table, blocks, dct_table, precision=lax.Precision.HIGHEST
    )
    return coeffs.reshape(-1)


def inverse_groups(flat_in, dct_table, row_count, columns):
    blocks = flat_in.reshape(row_count // 64, 64, columns // 64, 64)
    field_out = jnp.einsum(
        "kn,akbj,jm->anbm", dct_table, blocks, dct_table, precision=lax.Precision.HIGHEST
    )
    return field_out.reshape(row_count, columns)


def group_offsets(position, col_groups):
    group_id = jnp.arange(position.shape[0], dtype=jnp.int32)[:, None]
    return (
        group_id // col_groups * (4096 * col_groups)
        + position // 64 * (64 * col_groups)
        + group_id % col_groups * 64
        + position % 64
    )


def silu_slope(pre_act):
    sigma_h = jax.nn.sigmoid(pre_act)
    return sigma_h * (1.0 + pre_act * (1.0 - sigma_h))


def store_slot(saved, value, slot_clip, is_valid):
    previous = lax.dynamic_index_in_dim(saved, slot_clip, 0, keepdims=False)
    return lax.dynamic_update_index_in_dim(
        saved, jnp.where(is_valid, value, previous), slot_clip, 0
    )


def local(inputs, cotangent, weights, momentum, keep_index):
    sections = lax.axis_size("section")
    section_index = lax.axis_index("section")
    whole_inputs, whole_grads = (
        lax.all_gather(inputs, "section", axis=1, tiled=True),
        lax.all_gather(cotangent, "section", axis=1, tiled=True),
    )
    weight = weights[0]
    row_count, columns = weight.shape
    tok_dev = whole_inputs.shape[0]
    tok_mb = tok_dev // MICRO
    tick_count = MICRO + sections - 1
    first_in = whole_inputs.reshape(MICRO, tok_mb, columns)
    last_grad = whole_grads.reshape(MICRO, tok_mb, columns)

    def forward_tick(tick_idx, loop_state):
        incoming, saved_x, saved_a, saved_h = loop_state
        micro_slot = tick_idx - section_index
        is_valid = (micro_slot >= 0) & (micro_slot < MICRO)
        slot_clip = jnp.clip(micro_slot, 0, MICRO - 1)
        own_first = lax.dynamic_index_in_dim(first_in, slot_clip, 0, keepdims=False)
        activation = jnp.where(section_index == 0, own_first, incoming)
        pre_act = jnp.einsum("td,cd->tc", activation, weight, preferred_element_type=jnp.float32)
        gated_act = jax.nn.silu(pre_act).astype(jnp.bfloat16)
        result = (
            activation.astype(jnp.float32)
            + jnp.einsum("tc,cd->td", gated_act, weight, preferred_element_type=jnp.float32)
        ).astype(jnp.bfloat16)
        saved_x = store_slot(saved_x, activation, slot_clip, is_valid)
        saved_a = store_slot(saved_a, gated_act, slot_clip, is_valid)
        saved_h = store_slot(saved_h, pre_act, slot_clip, is_valid)
        outgoing = from_behind(result, "section", 1)
        return (outgoing, saved_x, saved_a, saved_h)

    start_state = (
        jnp.zeros((tok_mb, columns), jnp.bfloat16),
        jnp.zeros((MICRO, tok_mb, columns), jnp.bfloat16),
        jnp.zeros((MICRO, tok_mb, row_count), jnp.bfloat16),
        jnp.zeros((MICRO, tok_mb, row_count), jnp.float32),
    )
    loop_state = lax.fori_loop(0, tick_count, forward_tick, start_state)
    saved_x, saved_a, saved_h = (loop_state[1], loop_state[2], loop_state[3])

    def backward_tick(tick_idx, loop_state):
        incoming, saved_g, saved_d = loop_state
        micro_slot = tick_idx - (sections - 1 - section_index)
        is_valid = (micro_slot >= 0) & (micro_slot < MICRO)
        slot_clip = jnp.clip(micro_slot, 0, MICRO - 1)
        own_last = lax.dynamic_index_in_dim(last_grad, slot_clip, 0, keepdims=False)
        grad_in = jnp.where(section_index == sections - 1, own_last, incoming)
        pre_act = lax.dynamic_index_in_dim(saved_h, slot_clip, 0, keepdims=False)
        errors = jnp.einsum("td,cd->tc", grad_in, weight, preferred_element_type=jnp.float32)
        deltas = (errors * silu_slope(pre_act)).astype(jnp.bfloat16)
        saved_g = store_slot(saved_g, grad_in, slot_clip, is_valid)
        saved_d = store_slot(saved_d, deltas, slot_clip, is_valid)
        sent_back = (
            grad_in.astype(jnp.float32)
            + jnp.einsum("tc,cd->td", deltas, weight, preferred_element_type=jnp.float32)
        ).astype(jnp.bfloat16)
        outgoing = from_behind(sent_back, "section", -1)
        return (outgoing, saved_g, saved_d)

    back_state = (
        jnp.zeros((tok_mb, columns), jnp.bfloat16),
        jnp.zeros((MICRO, tok_mb, columns), jnp.bfloat16),
        jnp.zeros((MICRO, tok_mb, row_count), jnp.bfloat16),
    )
    back_out = lax.fori_loop(0, tick_count, backward_tick, back_state)
    saved_g = back_out[1].reshape(tok_dev, columns)
    saved_d = back_out[2].reshape(tok_dev, row_count)
    grad_total = jnp.einsum(
        "tc,td->cd",
        saved_a.reshape(tok_dev, row_count),
        saved_g,
        preferred_element_type=jnp.float32,
    )
    grad_total = grad_total + jnp.einsum(
        "tc,td->cd", saved_d, saved_x.reshape(tok_dev, columns), preferred_element_type=jnp.float32
    )
    dct_table = dct_basis(64)
    momentum_new = DECAY * momentum[0, 0].astype(jnp.float32) + grad_total
    coeffs = forward_groups(momentum_new, dct_table)
    offsets = group_offsets(keep_index[0, 0], columns // 64)
    kept_values = coeffs[offsets]
    own_sparse = jnp.zeros_like(coeffs).at[offsets.reshape(-1)].add(kept_values.reshape(-1))
    own_field = inverse_groups(own_sparse, dct_table, row_count, columns)
    momentum_out = (momentum_new - own_field).astype(jnp.bfloat16)
    update = lax.psum(own_field, "dp")
    return (momentum_out[None, None], update.astype(jnp.bfloat16)[None, None])


def solution(mesh):
    return jax.shard_map(
        local,
        mesh=mesh,
        in_specs=(
            P("dp", "section"),
            P("dp", "section"),
            P("section", None, None),
            P("section", "dp", None, None),
            P("section", "dp", None, None),
        ),
        out_specs=(P("section", "dp", None, None), P("section", "dp", None, None)),
        check_vma=False,
    )
```

profile of v0, /device:TPU:0, one launch (start us, length us, event | category | flops | bytes accessed | tf_op | source)
XLA Modules:
  0.0 467.1 jit_solution(12507494876444105098)
XLA Ops:
  10.7 34.7 %all-gather.3.cloned.1.call-done = bf16[128,8192]{1,0:T(8,128)(2,1)} async-done(((bf16[128,4096]{1,0:T(8,128)(2,1)}), bf16[128,8192]{1,0:T(8,128)(2,1)}) %all-gather.3.cloned.1.call-update) | async-done | bytes 2097168 | tf_op jit(solution)/shard_map/all_gather | solution.py:70
  46.3 116.0 %while.39 = (s32[]{:T(128)}, bf16[16,8192]{1,0:T(8,128)(2,1)}, bf16[8,16,8192]{2,1,0:T(8,128)(2,1)S(1)}, bf16[8,16,64]{2,1,0:T(8,128)(2,1)S(1)}, f32[8,16,64]{2,...) while((s32[]{:T(128)}, bf16[16,8192]{1,0:T(8,128)(2,1)}, ...), condition=%wide.region_1.2_spmd, body=%wide.region_0.1_spmd.sunk | while | flops 34222088 | bytes 6873366 | solution.py:106
  48.9 2.3 collective-permute-start
  51.3 8.7 %collective-permute-done = bf16[16,8192]{1,0:T(8,128)(2,1)S(1)} collective-permute-done((bf16[16,8192]{1,0:T(8,128)(2,1)}, bf16[16,8192]{1,0:T(8,128)(2,1)S(1)}, u32[]{:S(2)}, u32[]{:S(2)}) %collective-permute-start) | collective-permute-done | bytes 262176 | tf_op jit(solution)/shard_map/while/body/eval_jaxpr/ppermute | solution.py:17
  63.2 4.4 collective-permute-start
  67.6 11.2 %collective-permute-done = bf16[16,8192]{1,0:T(8,128)(2,1)S(1)} collective-permute-done((bf16[16,8192]{1,0:T(8,128)(2,1)}, bf16[16,8192]{1,0:T(8,128)(2,1)S(1)}, u32[]{:S(2)}, u32[]{:S(2)}) %collective-permute-start) | collective-permute-done | bytes 262176 | tf_op jit(solution)/shard_map/while/body/eval_jaxpr/ppermute | solution.py:17
  82.1 4.4 collective-permute-start
  86.5 4.3 collective-permute-done
  94.0 4.4 collective-permute-start
  98.4 4.1 collective-permute-done
  105.8 4.4 collective-permute-start
  110.2 4.1 collective-permute-done
  117.5 4.4 collective-permute-start
  121.9 4.1 collective-permute-done
  129.3 4.4 collective-permute-start
  133.7 4.1 collective-permute-done
  141.0 4.4 collective-permute-start
  145.4 4.4 collective-permute-done
  153.1 4.4 collective-permute-start
  157.5 4.1 collective-permute-done
  162.3 1.7 broadcast.361
  165.4 131.1 %while.40 = (s32[]{:T(128)}, bf16[16,8192]{1,0:T(8,128)(2,1)}, bf16[8,16,8192]{2,1,0:T(8,128)(2,1)}, bf16[8,16,64]{2,1,0:T(8,128)(2,1)}, pred[]{:T(512)}, /*inde...) while((s32[]{:T(128)}, bf16[16,8192]{1,0:T(8,128)(2,1)}, ...), condition=%wide.region_3.4_spmd, body=%wide.region_2.3_spmd.sunk | while | flops 34220040 | bytes 6834956 | solution.py:133
  167.0 1.9 bitcast_dynamic-update-slice_fusion.13
  170.1 1.3 collective-permute-start.1
  171.4 7.3 %collective-permute-done.1 = bf16[16,8192]{1,0:T(8,128)(2,1)S(1)} collective-permute-done((bf16[16,8192]{1,0:T(8,128)(2,1)S(1)}, bf16[16,8192]{1,0:T(8,128)(2,1)S(1)}, u32[]{:S(2)}, u32[]{:S(2)}) %collective-permute-start.1) | collective-permute-done | bytes 262176 | tf_op jit(solution)/shard_map/while/body/eval_jaxpr/ppermute | solution.py:17
  181.0 1.9 bitcast_dynamic-update-slice_fusion.13
  184.1 1.3 collective-permute-start.1
  185.5 8.4 %collective-permute-done.1 = bf16[16,8192]{1,0:T(8,128)(2,1)S(1)} collective-permute-done((bf16[16,8192]{1,0:T(8,128)(2,1)S(1)}, bf16[16,8192]{1,0:T(8,128)(2,1)S(1)}, u32[]{:S(2)}, u32[]{:S(2)}) %collective-permute-start.1) | collective-permute-done | bytes 262176 | tf_op jit(solution)/shard_map/while/body/eval_jaxpr/ppermute | solution.py:17
  196.2 1.8 bitcast_dynamic-update-slice_fusion.13
  199.3 1.3 collective-permute-start.1
  200.6 9.6 %collective-permute-done.1 = bf16[16,8192]{1,0:T(8,128)(2,1)S(1)} collective-permute-done((bf16[16,8192]{1,0:T(8,128)(2,1)S(1)}, bf16[16,8192]{1,0:T(8,128)(2,1)S(1)}, u32[]{:S(2)}, u32[]{:S(2)}) %collective-permute-start.1) | collective-permute-done | bytes 262176 | tf_op jit(solution)/shard_map/while/body/eval_jaxpr/ppermute | solution.py:17
  212.6 1.8 bitcast_dynamic-update-slice_fusion.13
  215.6 1.3 collective-permute-start.1
  216.9 8.9 %collective-permute-done.1 = bf16[16,8192]{1,0:T(8,128)(2,1)S(1)} collective-permute-done((bf16[16,8192]{1,0:T(8,128)(2,1)S(1)}, bf16[16,8192]{1,0:T(8,128)(2,1)S(1)}, u32[]{:S(2)}, u32[]{:S(2)}) %collective-permute-start.1) | collective-permute-done | bytes 262176 | tf_op jit(solution)/shard_map/while/body/eval_jaxpr/ppermute | solution.py:17
  228.2 1.8 bitcast_dynamic-update-slice_fusion.13
  231.3 1.3 collective-permute-start.1
  232.6 8.1 %collective-permute-done.1 = bf16[16,8192]{1,0:T(8,128)(2,1)S(1)} collective-permute-done((bf16[16,8192]{1,0:T(8,128)(2,1)S(1)}, bf16[16,8192]{1,0:T(8,128)(2,1)S(1)}, u32[]{:S(2)}, u32[]{:S(2)}) %collective-permute-start.1) | collective-permute-done | bytes 262176 | tf_op jit(solution)/shard_map/while/body/eval_jaxpr/ppermute | solution.py:17
  243.0 1.8 bitcast_dynamic-update-slice_fusion.13
  246.1 1.3 collective-permute-start.1
  247.4 7.2 %collective-permute-done.1 = bf16[16,8192]{1,0:T(8,128)(2,1)S(1)} collective-permute-done((bf16[16,8192]{1,0:T(8,128)(2,1)S(1)}, bf16[16,8192]{1,0:T(8,128)(2,1)S(1)}, u32[]{:S(2)}, u32[]{:S(2)}) %collective-permute-start.1) | collective-permute-done | bytes 262176 | tf_op jit(solution)/shard_map/while/body/eval_jaxpr/ppermute | solution.py:17
  257.0 1.8 bitcast_dynamic-update-slice_fusion.13
  260.0 1.3 collective-permute-start.1
  261.3 7.0 %collective-permute-done.1 = bf16[16,8192]{1,0:T(8,128)(2,1)S(1)} collective-permute-done((bf16[16,8192]{1,0:T(8,128)(2,1)S(1)}, bf16[16,8192]{1,0:T(8,128)(2,1)S(1)}, u32[]{:S(2)}, u32[]{:S(2)}) %collective-permute-start.1) | collective-permute-done | bytes 262176 | tf_op jit(solution)/shard_map/while/body/eval_jaxpr/ppermute | solution.py:17
  270.7 1.8 bitcast_dynamic-update-slice_fusion.13
  275.0 7.0 %collective-permute-done.1 = bf16[16,8192]{1,0:T(8,128)(2,1)S(1)} collective-permute-done((bf16[16,8192]{1,0:T(8,128)(2,1)S(1)}, bf16[16,8192]{1,0:T(8,128)(2,1)S(1)}, u32[]{:S(2)}, u32[]{:S(2)}) %collective-permute-start.1) | collective-permute-done | bytes 262176 | tf_op jit(solution)/shard_map/while/body/eval_jaxpr/ppermute | solution.py:17
  284.4 1.8 bitcast_dynamic-update-slice_fusion.13
  288.7 7.0 %collective-permute-done.1 = bf16[16,8192]{1,0:T(8,128)(2,1)S(1)} collective-permute-done((bf16[16,8192]{1,0:T(8,128)(2,1)S(1)}, bf16[16,8192]{1,0:T(8,128)(2,1)S(1)}, u32[]{:S(2)}, u32[]{:S(2)}) %collective-permute-start.1) | collective-permute-done | bytes 262176 | tf_op jit(solution)/shard_map/while/body/eval_jaxpr/ppermute | solution.py:17
  296.4 2.2 convolution_bitcast_fusion.1
  299.8 3.0 reshape.406
  302.8 4.2 copy.14
  307.0 3.8 fusion.27
  310.8 3.5 fusion.14
  314.3 2.7 copy.11
  317.0 3.3 reshape.407
  320.3 23.0 %gather_fusion = f32[4096]{0:T(1024)S(1)} fusion(f32[524288]{0:T(1024)S(1)} %reshape.407, s32[4096]{0:T(1024)S(1)} %broadcast_clamp_fusion), kind=kCustom, calls=%fused_computation | custom fusion | bytes 49152 | tf_op jit(solution)/shard_map/gather | solution.py:149
  343.3 22.6 %scatter_custom_fusion = f32[524288]{0:T(1024)S(1)} fusion(s32[4096]{0:T(1024)S(1)} %bitcast.169, f32[4096]{0:T(1024)S(1)} %gather_fusion, f32[]{:T(128)} %constant.209.clone.1), kind=kCustom, calls=%fused_computation.46 | custom fusion | flops 4096 | bytes 2097156 | tf_op jit(solution)/shard_map/scatter-add | solution.py:150
  365.9 2.3 reshape.409
  368.2 3.5 copy.17
  371.7 2.2 fusion.25
  374.0 3.4 fusion.17
  377.4 2.7 copy.13
  380.1 5.0 %reshape.410 = f32[64,8192]{1,0:T(8,128)} reshape(f32[1,64,128,64]{3,2,1,0:T(8,128)} %copy.13) | data formatting | bytes 4194304 | tf_op jit(solution)/shard_map/reshape | solution.py:41
  385.1 2.7 fusion.20
  387.9 72.4 %all-reduce.1 = bf16[64,8192]{1,0:T(8,128)(2,1)} all-reduce(f32[64,8192]{1,0:T(8,128)} %reshape.410), channel_id=1, replica_groups=mesh['section'=2,'dp'=16] {'dp'}, use_global_device_ids=true, to_apply=%region_5.6 | all-reduce | flops 524288 | bytes 3145728 | tf_op jit(solution)/shard_map/psum | solution.py:153
  (183 shorter events, 70.8 us)
Async XLA Ops:
  7.2 2.6 copy-start.9
  7.2 38.2 %all-gather.3.cloned.1.call-start = ((), (), s32[]{:S(2)}) async-start(), calls=%async_computation | async-start | bytes 3145728 | tf_op jit(solution)/shard_map/all_gather | solution.py:70
  7.9 38.4 %copy-start = (bf16[1,64,8192]{2,1,0:T(8,128)(2,1)S(1)}, bf16[1,64,8192]{2,1,0:T(8,128)(2,1)}, u32[]{:S(2)}) copy-start(bf16[1,64,8192]{2,1,0:T(8,128)(2,1)} %param.11) | copy-start | bytes 3145732
  7.9 154.4 %all-gather.5.cloned.1.call-start = ((), (), s32[]{:S(2)}) async-start(), calls=%async_computation.1 | async-start | bytes 3145728 | tf_op jit(solution)/shard_map/all_gather | solution.py:71
  48.9 11.1 %collective-permute-start = (bf16[16,8192]{1,0:T(8,128)(2,1)}, bf16[16,8192]{1,0:T(8,128)(2,1)S(1)}, u32[]{:S(2)}, u32[]{:S(2)}) collective-permute-start(bf16[16,8192]{1,0:T(8,128)(2,1)} %fusion.98), channel_id=1, source_target_pairs={{0,16},{1,17},{2,18},{3,19},{4,20},{5,21},{6,22},{7,23},{8,24},{9,... | collective-permute-start | bytes 786440 | tf_op jit(solution)/shard_map/while/body/eval_jaxpr/ppermute | solution.py:17
  60.0 0.7 copy-start.5
  63.2 15.6 %collective-permute-start = (bf16[16,8192]{1,0:T(8,128)(2,1)}, bf16[16,8192]{1,0:T(8,128)(2,1)S(1)}, u32[]{:S(2)}, u32[]{:S(2)}) collective-permute-start(bf16[16,8192]{1,0:T(8,128)(2,1)} %fusion.98), channel_id=1, source_target_pairs={{0,16},{1,17},{2,18},{3,19},{4,20},{5,21},{6,22},{7,23},{8,24},{9,... | collective-permute-start | bytes 786440 | tf_op jit(solution)/shard_map/while/body/eval_jaxpr/ppermute | solution.py:17
  78.8 0.7 copy-start.5
  82.1 8.7 %collective-permute-start = (bf16[16,8192]{1,0:T(8,128)(2,1)}, bf16[16,8192]{1,0:T(8,128)(2,1)S(1)}, u32[]{:S(2)}, u32[]{:S(2)}) collective-permute-start(bf16[16,8192]{1,0:T(8,128)(2,1)} %fusion.98), channel_id=1, source_target_pairs={{0,16},{1,17},{2,18},{3,19},{4,20},{5,21},{6,22},{7,23},{8,24},{9,... | collective-permute-start | bytes 786440 | tf_op jit(solution)/shard_map/while/body/eval_jaxpr/ppermute | solution.py:17
  90.8 0.7 copy-start.5
  94.0 8.5 %collective-permute-start = (bf16[16,8192]{1,0:T(8,128)(2,1)}, bf16[16,8192]{1,0:T(8,128)(2,1)S(1)}, u32[]{:S(2)}, u32[]{:S(2)}) collective-permute-start(bf16[16,8192]{1,0:T(8,128)(2,1)} %fusion.98), channel_id=1, source_target_pairs={{0,16},{1,17},{2,18},{3,19},{4,20},{5,21},{6,22},{7,23},{8,24},{9,... | collective-permute-start | bytes 786440 | tf_op jit(solution)/shard_map/while/body/eval_jaxpr/ppermute | solution.py:17
  102.6 0.7 copy-start.5
  105.8 8.5 %collective-permute-start = (bf16[16,8192]{1,0:T(8,128)(2,1)}, bf16[16,8192]{1,0:T(8,128)(2,1)S(1)}, u32[]{:S(2)}, u32[]{:S(2)}) collective-permute-start(bf16[16,8192]{1,0:T(8,128)(2,1)} %fusion.98), channel_id=1, source_target_pairs={{0,16},{1,17},{2,18},{3,19},{4,20},{5,21},{6,22},{7,23},{8,24},{9,... | collective-permute-start | bytes 786440 | tf_op jit(solution)/shard_map/while/body/eval_jaxpr/ppermute | solution.py:17
  114.3 0.7 copy-start.5
  117.5 8.5 %collective-permute-start = (bf16[16,8192]{1,0:T(8,128)(2,1)}, bf16[16,8192]{1,0:T(8,128)(2,1)S(1)}, u32[]{:S(2)}, u32[]{:S(2)}) collective-permute-start(bf16[16,8192]{1,0:T(8,128)(2,1)} %fusion.98), channel_id=1, source_target_pairs={{0,16},{1,17},{2,18},{3,19},{4,20},{5,21},{6,22},{7,23},{8,24},{9,... | collective-permute-start | bytes 786440 | tf_op jit(solution)/shard_map/while/body/eval_jaxpr/ppermute | solution.py:17
  126.1 0.7 copy-start.5
  129.3 8.5 %collective-permute-start = (bf16[16,8192]{1,0:T(8,128)(2,1)}, bf16[16,8192]{1,0:T(8,128)(2,1)S(1)}, u32[]{:S(2)}, u32[]{:S(2)}) collective-permute-start(bf16[16,8192]{1,0:T(8,128)(2,1)} %fusion.98), channel_id=1, source_target_pairs={{0,16},{1,17},{2,18},{3,19},{4,20},{5,21},{6,22},{7,23},{8,24},{9,... | collective-permute-start | bytes 786440 | tf_op jit(solution)/shard_map/while/body/eval_jaxpr/ppermute | solution.py:17
  137.8 0.7 copy-start.5
  141.0 8.8 %collective-permute-start = (bf16[16,8192]{1,0:T(8,128)(2,1)}, bf16[16,8192]{1,0:T(8,128)(2,1)S(1)}, u32[]{:S(2)}, u32[]{:S(2)}) collective-permute-start(bf16[16,8192]{1,0:T(8,128)(2,1)} %fusion.98), channel_id=1, source_target_pairs={{0,16},{1,17},{2,18},{3,19},{4,20},{5,21},{6,22},{7,23},{8,24},{9,... | collective-permute-start | bytes 786440 | tf_op jit(solution)/shard_map/while/body/eval_jaxpr/ppermute | solution.py:17
  149.8 0.7 copy-start.5
  153.1 8.5 %collective-permute-start = (bf16[16,8192]{1,0:T(8,128)(2,1)}, bf16[16,8192]{1,0:T(8,128)(2,1)S(1)}, u32[]{:S(2)}, u32[]{:S(2)}) collective-permute-start(bf16[16,8192]{1,0:T(8,128)(2,1)} %fusion.98), channel_id=1, source_target_pairs={{0,16},{1,17},{2,18},{3,19},{4,20},{5,21},{6,22},{7,23},{8,24},{9,... | collective-permute-start | bytes 786440 | tf_op jit(solution)/shard_map/while/body/eval_jaxpr/ppermute | solution.py:17
  161.6 0.7 copy-start.5
  162.3 3.1 copy-start.3
  170.1 8.6 %collective-permute-start.1 = (bf16[16,8192]{1,0:T(8,128)(2,1)S(1)}, bf16[16,8192]{1,0:T(8,128)(2,1)S(1)}, u32[]{:S(2)}, u32[]{:S(2)}) collective-permute-start(bf16[16,8192]{1,0:T(8,128)(2,1)S(1)} %fusion.103), channel_id=1, source_target_pairs={{16,0},{17,1},{18,2},{19,3},{20,4},{21,5},{22,6},{23,7},{24,8},{25... | collective-permute-start | bytes 786440 | tf_op jit(solution)/shard_map/while/body/eval_jaxpr/ppermute | solution.py:17
  178.7 0.7 copy-start.6
  184.1 9.7 %collective-permute-start.1 = (bf16[16,8192]{1,0:T(8,128)(2,1)S(1)}, bf16[16,8192]{1,0:T(8,128)(2,1)S(1)}, u32[]{:S(2)}, u32[]{:S(2)}) collective-permute-start(bf16[16,8192]{1,0:T(8,128)(2,1)S(1)} %fusion.103), channel_id=1, source_target_pairs={{16,0},{17,1},{18,2},{19,3},{20,4},{21,5},{22,6},{23,7},{24,8},{25... | collective-permute-start | bytes 786440 | tf_op jit(solution)/shard_map/while/body/eval_jaxpr/ppermute | solution.py:17
  193.9 0.7 copy-start.6
  199.3 10.9 %collective-permute-start.1 = (bf16[16,8192]{1,0:T(8,128)(2,1)S(1)}, bf16[16,8192]{1,0:T(8,128)(2,1)S(1)}, u32[]{:S(2)}, u32[]{:S(2)}) collective-permute-start(bf16[16,8192]{1,0:T(8,128)(2,1)S(1)} %fusion.103), channel_id=1, source_target_pairs={{16,0},{17,1},{18,2},{19,3},{20,4},{21,5},{22,6},{23,7},{24,8},{25... | collective-permute-start | bytes 786440 | tf_op jit(solution)/shard_map/while/body/eval_jaxpr/ppermute | solution.py:17
  210.2 0.7 copy-start.6
  215.6 10.2 %collective-permute-start.1 = (bf16[16,8192]{1,0:T(8,128)(2,1)S(1)}, bf16[16,8192]{1,0:T(8,128)(2,1)S(1)}, u32[]{:S(2)}, u32[]{:S(2)}) collective-permute-start(bf16[16,8192]{1,0:T(8,128)(2,1)S(1)} %fusion.103), channel_id=1, source_target_pairs={{16,0},{17,1},{18,2},{19,3},{20,4},{21,5},{22,6},{23,7},{24,8},{25... | collective-permute-start | bytes 786440 | tf_op jit(solution)/shard_map/while/body/eval_jaxpr/ppermute | solution.py:17
  225.8 0.7 copy-start.6
  231.3 9.4 %collective-permute-start.1 = (bf16[16,8192]{1,0:T(8,128)(2,1)S(1)}, bf16[16,8192]{1,0:T(8,128)(2,1)S(1)}, u32[]{:S(2)}, u32[]{:S(2)}) collective-permute-start(bf16[16,8192]{1,0:T(8,128)(2,1)S(1)} %fusion.103), channel_id=1, source_target_pairs={{16,0},{17,1},{18,2},{19,3},{20,4},{21,5},{22,6},{23,7},{24,8},{25... | collective-permute-start | bytes 786440 | tf_op jit(solution)/shard_map/while/body/eval_jaxpr/ppermute | solution.py:17
  240.6 0.7 copy-start.6
  246.1 8.5 %collective-permute-start.1 = (bf16[16,8192]{1,0:T(8,128)(2,1)S(1)}, bf16[16,8192]{1,0:T(8,128)(2,1)S(1)}, u32[]{:S(2)}, u32[]{:S(2)}) collective-permute-start(bf16[16,8192]{1,0:T(8,128)(2,1)S(1)} %fusion.103), channel_id=1, source_target_pairs={{16,0},{17,1},{18,2},{19,3},{20,4},{21,5},{22,6},{23,7},{24,8},{25... | collective-permute-start | bytes 786440 | tf_op jit(solution)/shard_map/while/body/eval_jaxpr/ppermute | solution.py:17
  254.6 0.7 copy-start.6
  260.0 8.3 %collective-permute-start.1 = (bf16[16,8192]{1,0:T(8,128)(2,1)S(1)}, bf16[16,8192]{1,0:T(8,128)(2,1)S(1)}, u32[]{:S(2)}, u32[]{:S(2)}) collective-permute-start(bf16[16,8192]{1,0:T(8,128)(2,1)S(1)} %fusion.103), channel_id=1, source_target_pairs={{16,0},{17,1},{18,2},{19,3},{20,4},{21,5},{22,6},{23,7},{24,8},{25... | collective-permute-start | bytes 786440 | tf_op jit(solution)/shard_map/while/body/eval_jaxpr/ppermute | solution.py:17
  268.3 0.7 copy-start.6
  273.7 8.3 %collective-permute-start.1 = (bf16[16,8192]{1,0:T(8,128)(2,1)S(1)}, bf16[16,8192]{1,0:T(8,128)(2,1)S(1)}, u32[]{:S(2)}, u32[]{:S(2)}) collective-permute-start(bf16[16,8192]{1,0:T(8,128)(2,1)S(1)} %fusion.103), channel_id=1, source_target_pairs={{16,0},{17,1},{18,2},{19,3},{20,4},{21,5},{22,6},{23,7},{24,8},{25... | collective-permute-start | bytes 786440 | tf_op jit(solution)/shard_map/while/body/eval_jaxpr/ppermute | solution.py:17
  282.0 0.7 copy-start.6
  287.4 8.3 %collective-permute-start.1 = (bf16[16,8192]{1,0:T(8,128)(2,1)S(1)}, bf16[16,8192]{1,0:T(8,128)(2,1)S(1)}, u32[]{:S(2)}, u32[]{:S(2)}) collective-permute-start(bf16[16,8192]{1,0:T(8,128)(2,1)S(1)} %fusion.103), channel_id=1, source_target_pairs={{16,0},{17,1},{18,2},{19,3},{20,4},{21,5},{22,6},{23,7},{24,8},{25... | collective-permute-start | bytes 786440 | tf_op jit(solution)/shard_map/while/body/eval_jaxpr/ppermute | solution.py:17
  295.7 0.7 copy-start.6
  296.4 2.2 copy-start.4
  296.4 2.5 copy-start.7
  296.4 2.5 copy-start.8
  299.8 3.0 copy-start.1
  302.8 4.2 copy-start.10
  302.8 4.2 copy-start.11
  380.1 5.0 %copy-start.2 = (f32[64,8192]{1,0:T(8,128)S(1)}, f32[64,8192]{1,0:T(8,128)}, u32[]{:S(2)}) copy-start(f32[64,8192]{1,0:T(8,128)} %copy-done.1) | copy-start | bytes 6291460
Sparse Core Ops, SparseCore 0:
  9.5 35.8 all-gather.2
  46.9 39.2 all-gather.4
where the time goes:
time: 469 us; the launch traced here: 467 us
  waiting for transfers between devices  156 us (33%)
  local copies, waits for them, and re-layouts  82.7 us (18%)
  blocking collectives  72.4 us (15%)
  other arithmetic  52.9 us (11%)
  starting transfers between devices  48.9 us (10%)
  matrix products  39.7 us (8%)
  between operations  14.2 us (3%)
    ppermute x18, waiting for transfers between devices, from_behind(): lax.ppermute(value, axis, [(source, source + steps) for source in range(l...  120 us
    psum x1, blocking collectives, local(): update = lax.psum(own_field, 'dp')  72.4 us
    ppermute x18, starting transfers between devices, from_behind(): lax.ppermute(value, axis, [(source, source + steps) for source in range(l...  48.8 us
    all_gather x1, waiting for transfers between devices, local(): lax.all_gather(inputs, 'section', axis=1, tiled=True)  34.7 us
    dynamic_update_slice x27, other arithmetic, store_slot(): lax.dynamic_update_index_in_dim(saved, jnp.where(is_valid, value, previou...  26.2 us
    gather x1, local copies, waits for them, and re-layouts, local(): kept_values = coeffs[offsets]  23 us
    scatter-add x1, other arithmetic, local(): jnp.zeros_like(coeffs).at[offsets.reshape(-1)].add(kept_values.reshape(-1))  22.6 us
    dynamic_slice x45, local copies, waits for them, and re-layouts, store_slot(): previous = lax.dynamic_index_in_dim(saved, slot_clip, 0, keepdims=False)  15.3 us
  transfers between devices with their start and end apart: 20, of which 19 were waited for; matrix products, arithmetic and copies ran while one was open for 5% of the time, Pallas kernels for 0%

commit v1 on v0

v1 whole, which is shorter than its diff:
```python
import functools
import math

import jax
import jax.numpy as jnp
import numpy as np
from jax import lax
from jax.experimental import pallas as pl
from jax.experimental.pallas import tpu as pltpu
from jax.sharding import PartitionSpec as P

DECAY = 0.999
BLOCK = 64
TILE = 256
F32 = jnp.float32
BF16 = jnp.bfloat16
VMEM = pl.BlockSpec(memory_space=pltpu.VMEM)
NT = (((1,), (1,)), ((), ()))
TN = (((0,), (0,)), ((), ()))
NN = (((1,), (0,)), ((), ()))


def dot(left, right, dims=NN):
    return lax.dot_general(left, right, dims, preferred_element_type=F32)


def dot_full(left, right, dims=NN):
    return lax.dot_general(
        left, right, dims, precision=lax.Precision.HIGHEST, preferred_element_type=F32
    )


def split(value):
    high = value.astype(BF16)
    return high, (value - high.astype(F32)).astype(BF16)


def np_basis():
    freq = np.arange(BLOCK)[:, None]
    position = np.arange(BLOCK)[None, :]
    table = np.cos(math.pi * (position + 0.5) * freq / BLOCK) * math.sqrt(2.0 / BLOCK)
    return np.where(freq == 0, table * math.sqrt(0.5), table)


def np_split(table):
    high = table.astype(np.float32).astype(jnp.bfloat16)
    low = (table - high.astype(np.float64)).astype(np.float32).astype(jnp.bfloat16)
    return high, low


def tables(inverse):
    basis = np_basis()
    left = basis.T if inverse else basis
    right = np.kron(np.eye(TILE // BLOCK), basis if inverse else basis.T)
    left_high, left_low = np_split(left)
    right_high, right_low = np_split(right)
    left_all = np.concatenate([left_high, left_low, left_high], axis=1)
    return [jnp.asarray(left_all), jnp.asarray(right_high), jnp.asarray(right_low)]


def two_sided(value, left_all, right_high, right_low):
    high, low = split(value)
    mid = dot(high, right_high) + dot(low, right_high) + dot(high, right_low)
    high, low = split(mid)
    return dot(left_all, jnp.concatenate([high, high, low], axis=0))


def silu_slope(pre_act):
    sigma_h = 1.0 / (1.0 + jnp.exp(-pre_act))
    return sigma_h * (1.0 + pre_act * (1.0 - sigma_h))


def silu(v):
    return v / (1.0 + jnp.exp(-v))


def grads_kernel(layers, sums_ref, x_ref, g_ref, w_ref, out_ref):
    tokens, columns = x_ref.shape
    rows = w_ref.shape[0] // layers
    sums = sums_ref[...]

    def of(base, count, layer):
        return sums[base : base + count, layer * rows : (layer + 1) * rows]

    def gram(m, l):
        return of(2 * tokens + m * rows, rows, l)

    pre, acts = [], []
    for l in range(layers):
        h = of(0, tokens, l)
        for m in range(l):
            h = h + dot_full(acts[m].astype(F32), gram(m, l))
        pre.append(h)
        acts.append(silu(h).astype(BF16))
    deltas = [None] * layers
    for l in reversed(range(layers)):
        e = of(tokens, tokens, l)
        for m in range(l + 1, layers):
            e = e + dot_full(deltas[m].astype(F32), gram(m, l))
        deltas[l] = (e * silu_slope(pre[l])).astype(BF16)
    a_t = jnp.concatenate([a.astype(F32).T for a in acts], axis=0).astype(BF16)
    d_t = jnp.concatenate([d.astype(F32).T for d in deltas], axis=0).astype(BF16)
    row = lax.broadcasted_iota(jnp.int32, (layers * rows, layers * rows), 0) // rows
    col = lax.broadcasted_iota(jnp.int32, (layers * rows, layers * rows), 1) // rows
    a_d = dot(a_t, d_t, NT)
    d_a = dot(d_t, a_t, NT)
    cross = jnp.where(col > row, a_d, jnp.where(col < row, d_a, 0.0))
    cross_high, cross_low = split(cross)

    def body(i, carry):
        at = pl.ds(pl.multiple_of(i * TILE, TILE), TILE)
        w = w_ref[:, at]
        total = dot(a_t, g_ref[:, at]) + dot(d_t, x_ref[:, at])
        total = total + dot(cross_high, w) + dot(cross_low, w)
        out_ref[:, at] = total.astype(BF16)
        return carry

    lax.fori_loop(0, columns // TILE, body, 0)


def encode_kernel(momentum_ref, grad_ref, index_ref, fl, frh, frl, il, irh, irl, out_ref, kept_ref):
    columns = momentum_ref.shape[1]
    per = TILE // BLOCK
    entries = index_ref.shape[1]
    forward = (fl[...], frh[...], frl[...])
    inverse = (il[...], irh[...], irl[...])
    lane_block = lax.broadcasted_iota(jnp.int32, (1, entries), 1) // (entries // per)
    k_iota = lax.broadcasted_iota(jnp.int32, (BLOCK, entries), 0)
    j_iota = lax.broadcasted_iota(jnp.int32, (TILE, entries), 0)

    def body(i, carry):
        at = pl.ds(pl.multiple_of(i * TILE, TILE), TILE)
        fresh = DECAY * momentum_ref[:, at].astype(F32) + grad_ref[:, at].astype(F32)
        coef = two_sided(fresh, *forward)
        index = index_ref[pl.ds(i, 1), :]
        k_hot = jnp.where(k_iota == index >> 6, 1.0, 0.0)
        j_hot = jnp.where(j_iota == (index & 63) + lane_block * BLOCK, 1.0, 0.0).astype(BF16)
        mask = dot(k_hot.astype(BF16), j_hot, NT)
        picked = dot(coef.astype(BF16), j_hot)
        kept_ref[pl.ds(i, 1), :] = jnp.sum(picked * k_hot, axis=0, keepdims=True)
        out_ref[:, at] = (fresh - two_sided(coef * mask, *inverse)).astype(BF16)
        return carry

    lax.fori_loop(0, columns // TILE, body, 0)


def decode_kernel(kept_ref, index_ref, il, irh, irl, out_ref):
    columns = out_ref.shape[1]
    per = TILE // BLOCK
    entries = index_ref.shape[2]
    inverse = (il[...], irh[...], irl[...])
    iota = lax.broadcasted_iota(jnp.int32, (BLOCK, entries), 0)

    def body(i, carry):
        at = pl.ds(pl.multiple_of(i * TILE, TILE), TILE)
        indices = index_ref[i]
        values = kept_ref[i].astype(F32)
        blocks = []
        for b in range(per):
            index = indices[b : b + 1, :]
            kept = values[b : b + 1, :]
            k_hot = jnp.where(iota == index >> 6, kept, 0.0).astype(BF16)
            j_hot = jnp.where(iota == (index & 63), 1.0, 0.0).astype(BF16)
            blocks.append(dot(k_hot, j_hot, NT))
        out_ref[:, at] = two_sided(jnp.concatenate(blocks, axis=1), *inverse).astype(BF16)
        return carry

    lax.fori_loop(0, columns // TILE, body, 0)


def call(kernel, out_shape, *args):
    return pl.pallas_call(
        kernel,
        out_shape=out_shape,
        in_specs=[VMEM] * len(args),
        out_specs=jax.tree.map(lambda _: VMEM, out_shape),
        cost_estimate=pl.CostEstimate(flops=10**9, bytes_accessed=4 * 2**20, transcendentals=0),
    )(*args)


def shifts(axis):
    count = lax.axis_size(axis)
    for step in range(1, count):
        yield step, [(source, (source + step) % count) for source in range(count)]


def exchange(parts, own, axis="section"):
    count = lax.axis_size(axis)
    me = lax.axis_index(axis)
    stacked = jnp.broadcast_to(own[None], (count,) + own.shape)
    for step, pairs in shifts(axis):
        got = lax.ppermute(parts((me + step) % count), axis, pairs)
        source = (me + count - step) % count
        if count == 2:
            slot = lax.broadcasted_iota(jnp.int32, (count,) + (1,) * own.ndim, 0)
            stacked = jnp.where(slot == source, got[None], stacked)
        else:
            stacked = lax.dynamic_update_index_in_dim(stacked, got, source, 0)
    return stacked


def local(inputs, cotangent, weights, momentum, keep_index):
    layers = lax.axis_size("section")
    replicas = lax.axis_size("dp")
    me = lax.axis_index("section")
    rows, width = weights.shape[1:]
    columns = inputs.shape[1]
    groups, kept_count = keep_index.shape[2:]
    weight = weights[0]
    per = TILE // BLOCK

    index_all = lax.all_gather(keep_index[0, 0], "dp")
    index_all = index_all.transpose(1, 0, 2).reshape(groups // per, per, replicas * kept_count)

    def columns_of(i):
        return lax.dynamic_slice_in_dim(weight, i * columns, columns, 1)

    window = exchange(columns_of, columns_of(me)).reshape(layers * rows, columns)
    stack = jnp.concatenate([inputs, cotangent, window], axis=0)
    sums = lax.dot_general(stack, window, NT, preferred_element_type=F32)
    total = sums
    for _, pairs in shifts("section"):
        total = total + lax.ppermute(sums, "section", pairs)

    grads = call(
        functools.partial(grads_kernel, layers),
        jax.ShapeDtypeStruct((layers * rows, columns), BF16),
        total, inputs, cotangent, window,
    ).reshape(layers, rows, columns)

    def grad_of(i):
        return lax.dynamic_index_in_dim(grads, i, 0, keepdims=False)

    grad = exchange(grad_of, grad_of(me)).transpose(1, 0, 2).reshape(rows, width)
    index = keep_index[0, 0].reshape(groups // per, per * kept_count)
    inverse = tables(True)
    momentum_out, kept = call(
        encode_kernel,
        (
            jax.ShapeDtypeStruct((rows, width), BF16),
            jax.ShapeDtypeStruct((groups // per, per * kept_count), F32),
        ),
        momentum[0, 0], grad, index, *tables(False), *inverse,
    )
    kept_all = lax.all_gather(kept.astype(BF16), "dp")
    kept_all = kept_all.reshape(replicas, groups, kept_count).transpose(1, 0, 2)
    update = call(
        decode_kernel,
        jax.ShapeDtypeStruct((rows, width), BF16),
        kept_all.reshape(index_all.shape), index_all, *inverse,
    )
    return momentum_out[None, None], update[None, None]


def solution(mesh):
    return jax.shard_map(
        local,
        mesh=mesh,
        in_specs=(
            P("dp", "section"),
            P("dp", "section"),
            P("section", None, None),
            P("section", "dp", None, None),
            P("section", "dp", None, None),
        ),
        out_specs=(P("section", "dp", None, None), P("section", "dp", None, None)),
        check_vma=False,
    )
```

time: 469 us -> 134 us (0.29)
  waiting for transfers between devices: 156 us -> 16.1 us
  local copies, waits for them, and re-layouts: 82.7 us -> 11.4 us
  Pallas kernels: 0 us -> 55.7 us
  other arithmetic: 52.9 us -> 2.68 us
  starting transfers between devices: 48.9 us -> 6.36 us
  matrix products: 39.7 us -> 1.01 us
  blocking collectives: 72.4 us -> 40.1 us
  between operations: 14.2 us -> 0.76 us
    ppermute x18 -> x3, waiting for transfers between devices: 120 us -> 16.1 us  [the longest x2 11.8 us: exchange(): got = lax.ppermute(parts((me + step) % count), axis, pairs)]
    psum x1 -> x0, blocking collectives: 72.4 us -> none  [local(): update = lax.psum(own_field, 'dp')]
    pallas_call x0 -> x3, Pallas kernels: none -> 55.7 us  [call(): pl.pallas_call(kernel, out_shape=out_shape, in_specs=[VMEM] * len(args),...]
    ppermute x18 -> x3, starting transfers between devices: 48.8 us -> 6.36 us  [the longest x2 4.56 us: exchange(): got = lax.ppermute(parts((me + step) % count), axis, pairs)]
    all_gather x0 -> x2, blocking collectives: none -> 40.1 us  [the longest x1 22.3 us: local(): index_all = lax.all_gather(keep_index[0, 0], 'dp')]
    dot_general x42 -> x1, matrix products: 39.7 us -> 1.01 us  [local(): sums = lax.dot_general(stack, window, NT, preferred_element_type=F32)]
    all_gather x2 -> x0, waiting for transfers between devices: 34.7 us -> none  [the longest x1 34.7 us: local(): lax.all_gather(inputs, 'section', axis=1, tiled=True)]
    dynamic_update_slice x27 -> x0, other arithmetic: 26.2 us -> none  [store_slot(): lax.dynamic_update_index_in_dim(saved, jnp.where(is_valid, value, previou...]
  transfers between devices with their start and end apart: 20 -> 3, of which waited for: 19 -> 2; matrix products, arithmetic and copies ran while one was open for 5% -> 3% of each run, Pallas kernels for 0% -> 0%
where the time goes in v1:
time: 134 us
  Pallas kernels  55.7 us (42%)
  blocking collectives  40.1 us (30%)
  waiting for transfers between devices  16.1 us (12%)
  local copies, waits for them, and re-layouts  11.4 us (9%)
  starting transfers between devices  6.36 us (5%)
  other arithmetic  2.68 us (2%)
    pallas_call x3, Pallas kernels, call(): pl.pallas_call(kernel, out_shape=out_shape, in_specs=[VMEM] * len(args),...  55.7 us
    all_gather x1, blocking collectives, local(): index_all = lax.all_gather(keep_index[0, 0], 'dp')  22.3 us
    all_gather x1, blocking collectives, local(): kept_all = lax.all_gather(kept.astype(BF16), 'dp')  17.8 us
    ppermute x2, waiting for transfers between devices, exchange(): got = lax.ppermute(parts((me + step) % count), axis, pairs)  11.8 us
    ppermute x2, starting transfers between devices, exchange(): got = lax.ppermute(parts((me + step) % count), axis, pairs)  4.56 us
    ppermute x1, waiting for transfers between devices, local(): total = total + lax.ppermute(sums, 'section', pairs)  4.33 us
  transfers between devices with their start and end apart: 3, of which 2 were waited for; matrix products, arithmetic and copies ran while one was open for 3% of the time, Pallas kernels for 0%

profile of v1, /device:TPU:0, one launch (start us, length us, event | category | flops | bytes accessed | tf_op | source)
XLA Modules:
  0.0 134.1 jit_solution(12314596953059043656)
XLA Ops:
  0.6 1.3 dynamic-slice_bitcast_fusion.3
  1.9 3.0 %collective-permute-start = (bf16[64,4096]{1,0:T(8,128)(2,1)S(1)}, bf16[64,4096]{1,0:T(8,128)(2,1)S(1)}, u32[]{:S(2)}, u32[]{:S(2)}) collective-permute-start(bf16[64,4096]{1,0:T(8,128)(2,1)S(1)} %get-tuple-element.8), channel_id=1, source_target_pairs={{0,16},{16,0},{1,17},{17,1},{2,18},{18,2},{3,19},{19,3},{4,20},{20... | collective-permute-start | bytes 1572872 | tf_op jit(solution)/shard_map/ppermute | solution.py:192
  5.0 0.1 broadcast_in_dim.69
  5.0 0.1 broadcast_in_dim.70
  5.1 11.8 %collective-permute-done = bf16[64,4096]{1,0:T(8,128)(2,1)S(1)} collective-permute-done((bf16[64,4096]{1,0:T(8,128)(2,1)S(1)}, bf16[64,4096]{1,0:T(8,128)(2,1)S(1)}, u32[]{:S(2)}, u32[]{:S(2)}) %collective-permute-start) | collective-permute-done | bytes 524320 | tf_op jit(solution)/shard_map/ppermute | solution.py:192
  16.9 0.0 copy-start.1
  16.9 0.0 copy-start.2
  16.9 0.2 bitcast_select_fusion.w_ref
  17.1 1.1 copy-done.1
  18.1 0.3 copy-done.2
  18.4 0.0 copy-start
  18.4 1.0 fusion
  19.4 0.0 copy-done
  19.4 1.8 %collective-permute-start.1 = (f32[384,128]{1,0:T(8,128)S(1)}, f32[384,128]{1,0:T(8,128)S(1)}, u32[]{:S(2)}, u32[]{:S(2)}) collective-permute-start(f32[384,128]{1,0:T(8,128)S(1)} %fusion), channel_id=1, source_target_pairs={{0,16},{16,0},{1,17},{17,1},{2,18},{18,2},{3,19},{19,3},{4,20},{20... | collective-permute-start | bytes 589832 | tf_op jit(solution)/shard_map/ppermute | solution.py:223
  21.3 4.3 %collective-permute-done.1 = f32[384,128]{1,0:T(8,128)S(1)} collective-permute-done((f32[384,128]{1,0:T(8,128)S(1)}, f32[384,128]{1,0:T(8,128)S(1)}, u32[]{:S(2)}, u32[]{:S(2)}) %collective-permute-start.1) | collective-permute-done | bytes 196640 | tf_op jit(solution)/shard_map/ppermute | solution.py:223
  25.6 0.7 add.33.sums_ref
  26.3 7.3 %shard_map.122 = bf16[128,4096]{1,0:T(8,128)(2,1)} custom-call(f32[384,128]{1,0:T(8,128)} %add.33.sums_ref, bf16[128,4096]{1,0:T(8,128)(2,1)} %x_ref.1, bf16[128,4096]{1,0:T(8,128)(2,1)} %g_ref.1, bf16[128,4096]{1,0:T(8,128)(2,1)} %copy-done), custom_call_target="tpu_custom_call" | custom-call | flops 1000000000 | bytes 4194304 | tf_op jit(solution)/shard_map/pallas_call | solution.py:172
  33.6 0.0 copy-start.3
  33.6 1.3 dynamic-slice_bitcast_fusion
  34.9 1.5 %collective-permute-start.2 = (bf16[64,4096]{1,0:T(8,128)(2,1)S(1)}, bf16[64,4096]{1,0:T(8,128)(2,1)S(1)}, u32[]{:S(2)}, u32[]{:S(2)}) collective-permute-start(bf16[64,4096]{1,0:T(8,128)(2,1)S(1)} %get-tuple-element.7), channel_id=1, source_target_pairs={{0,16},{16,0},{1,17},{17,1},{2,18},{18,2},{3,19},{19,3},{4,20},{20... | collective-permute-start | bytes 1572872 | tf_op jit(solution)/shard_map/ppermute | solution.py:192
  36.4 0.1 broadcast_in_dim.66
  36.5 0.0 copy-done.3
  36.5 0.1 copy.19
  36.6 0.7 reshape_squeeze.3.index_ref
  37.3 22.3 %all-gather.1 = s32[16,1,128,32]{2,3,1,0:T(8,128)S(1)} all-gather(s32[1,1,128,32]{2,3,1,0:T(8,128)S(1)} %copy-done.3), channel_id=3, replica_groups=mesh['section'=2,'dp'=16] {'dp'}, dimensions={0}, use_global_device_ids=true | all-gather | bytes 278528 | tf_op jit(solution)/shard_map/all_gather | solution.py:212
  59.6 0.5 copy.21
  60.1 1.1 reshape.37.index_ref
  61.3 1.0 broadcast_in_dim.80
  62.3 0.6 copy.23
  62.9 0.0 collective-permute-done.2
  62.9 1.0 broadcast_in_dim.77
  63.9 0.6 copy.22
  64.5 1.1 broadcast_select_fusion.grad_ref
  65.6 27.2 %shard_map.123 = (bf16[64,8192]{1,0:T(8,128)(2,1)}, f32[32,128]{1,0:T(8,128)}) custom-call(bf16[64,8192]{1,0:T(8,128)(2,1)} %bitcast.34, bf16[64,8192]{1,0:T(8,128)(2,1)} %broadcast_select_fusion.grad_ref, s32[32,128]{1,0:T(8,128)} %reshape_squeeze.3.index_ref, bf16[64,192]{1,0:T(8,128)(2,1)} %constant.58.clone.fl, bf16[256,256]{1,0:T(8,128)(2,1)} %constant.59.clone.frh, ...), custom_call_target="tpu_custom_call" | custom-call | flops 1000000000 | bytes 4194304 | tf_op jit(solution)/shard_map/pallas_call | solution.py:172
  92.8 0.7 convert_element_type.3
  93.5 17.8 %all-gather = bf16[512,128]{1,0:T(8,128)(2,1)S(1)} all-gather(bf16[32,128]{1,0:T(8,128)(2,1)S(1)} %convert_element_type.3), channel_id=2, replica_groups=mesh['section'=2,'dp'=16] {'dp'}, dimensions={0}, use_global_device_ids=true | all-gather | bytes 139264 | tf_op jit(solution)/shard_map/all_gather | solution.py:245
  111.3 0.2 reshape.35
  111.5 0.3 copy.20
  111.9 1.0 reshape.36.kept_ref
  112.9 21.1 %shard_map.124 = bf16[64,8192]{1,0:T(8,128)(2,1)} custom-call(bf16[32,4,512]{2,1,0:T(4,128)(2,1)} %reshape.36.kept_ref, s32[32,4,512]{2,1,0:T(4,128)} %reshape.37.index_ref, bf16[64,192]{1,0:T(8,128)(2,1)} %constant.55.clone.il, bf16[256,256]{1,0:T(8,128)(2,1)} %constant.56.clone.irh, bf16[256,256]{1,0:T(8,128)(2,1)} %constant.57.clone.irl), custom_call_target="tpu_custom_call" | custom-call | flops 1000000000 | bytes 4194304 | tf_op jit(solution)/shard_map/pallas_call | solution.py:172
  (2 shorter events, 0.0 us)
Async XLA Ops:
  1.9 15.0 %collective-permute-start = (bf16[64,4096]{1,0:T(8,128)(2,1)S(1)}, bf16[64,4096]{1,0:T(8,128)(2,1)S(1)}, u32[]{:S(2)}, u32[]{:S(2)}) collective-permute-start(bf16[64,4096]{1,0:T(8,128)(2,1)S(1)} %get-tuple-element.8), channel_id=1, source_target_pairs={{0,16},{16,0},{1,17},{17,1},{2,18},{18,2},{3,19},{19,3},{4,20},{20... | collective-permute-start | bytes 1572872 | tf_op jit(solution)/shard_map/ppermute | solution.py:192
  16.9 1.2 copy-start.1
  16.9 1.5 %copy-start.2 = (bf16[128,4096]{1,0:T(8,128)(2,1)S(1)}, bf16[128,4096]{1,0:T(8,128)(2,1)}, u32[]{:S(2)}) copy-start(bf16[128,4096]{1,0:T(8,128)(2,1)} %x_ref.1) | copy-start | bytes 3145732
  18.4 1.0 copy-start
  19.4 6.1 %collective-permute-start.1 = (f32[384,128]{1,0:T(8,128)S(1)}, f32[384,128]{1,0:T(8,128)S(1)}, u32[]{:S(2)}, u32[]{:S(2)}) collective-permute-start(f32[384,128]{1,0:T(8,128)S(1)} %fusion), channel_id=1, source_target_pairs={{0,16},{16,0},{1,17},{17,1},{2,18},{18,2},{3,19},{19,3},{4,20},{20... | collective-permute-start | bytes 589832 | tf_op jit(solution)/shard_map/ppermute | solution.py:223
  33.6 2.9 %copy-start.3 = (s32[1,1,128,32]{2,3,1,0:T(8,128)S(1)}, s32[1,1,128,32]{2,3,1,0:T(8,128)}, u32[]{:S(2)}) copy-start(s32[1,1,128,32]{2,3,1,0:T(8,128)} %param.15) | copy-start | bytes 49156
  34.9 28.0 %collective-permute-start.2 = (bf16[64,4096]{1,0:T(8,128)(2,1)S(1)}, bf16[64,4096]{1,0:T(8,128)(2,1)S(1)}, u32[]{:S(2)}, u32[]{:S(2)}) collective-permute-start(bf16[64,4096]{1,0:T(8,128)(2,1)S(1)} %get-tuple-element.7), channel_id=1, source_target_pairs={{0,16},{16,0},{1,17},{17,1},{2,18},{18,2},{3,19},{19,3},{4,20},{20... | collective-permute-start | bytes 1572872 | tf_op jit(solution)/shard_map/ppermute | solution.py:192

commit v2 on v1

v2 whole, which is shorter than its diff:
```python
import functools
import math

import jax
import jax.numpy as jnp
import numpy as np
from jax import lax
from jax.experimental import pallas as pl
from jax.experimental.pallas import tpu as pltpu
from jax.sharding import PartitionSpec as P

DECAY = 0.999
BLOCK = 64
TILE = 256
F32 = jnp.float32
BF16 = jnp.bfloat16
VMEM = pl.BlockSpec(memory_space=pltpu.VMEM)
NT = (((1,), (1,)), ((), ()))
TN = (((0,), (0,)), ((), ()))
NN = (((1,), (0,)), ((), ()))


def dot(left, right, dims=NN):
    return lax.dot_general(left, right, dims, preferred_element_type=F32)


def dot_full(left, right, dims=NN):
    return lax.dot_general(
        left, right, dims, precision=lax.Precision.HIGHEST, preferred_element_type=F32
    )


def split(value):
    high = value.astype(BF16)
    return high, (value - high.astype(F32)).astype(BF16)


def np_basis():
    freq = np.arange(BLOCK)[:, None]
    position = np.arange(BLOCK)[None, :]
    table = np.cos(math.pi * (position + 0.5) * freq / BLOCK) * math.sqrt(2.0 / BLOCK)
    return np.where(freq == 0, table * math.sqrt(0.5), table)


def np_split(table):
    high = table.astype(np.float32).astype(jnp.bfloat16)
    low = (table - high.astype(np.float64)).astype(np.float32).astype(jnp.bfloat16)
    return high, low


def tables(inverse):
    basis = np_basis()
    left = basis.T if inverse else basis
    right = np.kron(np.eye(TILE // BLOCK), basis if inverse else basis.T)
    left_high, left_low = np_split(left)
    right_high, right_low = np_split(right)
    left_all = np.concatenate([left_high, left_low, left_high], axis=1)
    return [jnp.asarray(left_all), jnp.asarray(right_high), jnp.asarray(right_low)]


def two_sided(values, left_all, right_high, right_low):
    high, low = split(jnp.concatenate(values, axis=0))
    mid = dot(high, right_high) + dot(low, right_high) + dot(high, right_low)
    high, low = split(mid)
    outs = []
    for u in range(len(values)):
        h, l = high[u * BLOCK : (u + 1) * BLOCK], low[u * BLOCK : (u + 1) * BLOCK]
        outs.append(dot(left_all, jnp.concatenate([h, h, l], axis=0)))
    return outs


def silu_slope(pre_act):
    sigma_h = 1.0 / (1.0 + jnp.exp(-pre_act))
    return sigma_h * (1.0 + pre_act * (1.0 - sigma_h))


def silu(v):
    return v / (1.0 + jnp.exp(-v))


def grads_kernel(layers, sums_ref, x_ref, g_ref, w_ref, out_ref):
    tokens, columns = x_ref.shape
    rows = w_ref.shape[0] // layers
    sums = sums_ref[...]

    def of(base, count, layer):
        return sums[base : base + count, layer * rows : (layer + 1) * rows]

    def gram(m, l):
        return of(2 * tokens + m * rows, rows, l)

    pre, acts = [], []
    for l in range(layers):
        h = of(0, tokens, l)
        for m in range(l):
            h = h + dot_full(acts[m].astype(F32), gram(m, l))
        pre.append(h)
        acts.append(silu(h).astype(BF16))
    deltas = [None] * layers
    for l in reversed(range(layers)):
        e = of(tokens, tokens, l)
        for m in range(l + 1, layers):
            e = e + dot_full(deltas[m].astype(F32), gram(m, l))
        deltas[l] = (e * silu_slope(pre[l])).astype(BF16)
    a_t = jnp.concatenate([a.astype(F32).T for a in acts], axis=0).astype(BF16)
    d_t = jnp.concatenate([d.astype(F32).T for d in deltas], axis=0).astype(BF16)
    row = lax.broadcasted_iota(jnp.int32, (layers * rows, layers * rows), 0) // rows
    col = lax.broadcasted_iota(jnp.int32, (layers * rows, layers * rows), 1) // rows
    a_d = dot(a_t, d_t, NT)
    d_a = dot(d_t, a_t, NT)
    cross = jnp.where(col > row, a_d, jnp.where(col < row, d_a, 0.0))
    cross_high, cross_low = split(cross)

    step = math.gcd(4 * TILE, columns)

    def body(i, carry):
        at = pl.ds(pl.multiple_of(i * step, step), step)
        w = w_ref[:, at]
        total = dot(a_t, g_ref[:, at]) + dot(d_t, x_ref[:, at])
        total = total + dot(cross_high, w) + dot(cross_low, w)
        out_ref[:, at] = total.astype(BF16)
        return carry

    lax.fori_loop(0, columns // step, body, 0)


def encode_tiles(count, first, momentum_at, grad_at, index_ref, table_refs, store):
    per = TILE // BLOCK
    entries = index_ref.shape[1]
    forward = [ref[...] for ref in table_refs[:3]]
    inverse = [ref[...] for ref in table_refs[3:]]
    lane_block = lax.broadcasted_iota(jnp.int32, (1, entries), 1) // (entries // per)
    k_iota = lax.broadcasted_iota(jnp.int32, (BLOCK, entries), 0)
    j_iota = lax.broadcasted_iota(jnp.int32, (TILE, entries), 0)
    unroll = math.gcd(8, count)

    def body(n, carry):
        tiles = [n * unroll + u for u in range(unroll)]
        fresh = [DECAY * momentum_at(i).astype(F32) + grad_at(i).astype(F32) for i in tiles]
        coefs = two_sided(fresh, *forward)
        masked, rows = [], []
        for i, coef in zip(tiles, coefs):
            index = index_ref[pl.ds(first + i, 1), :]
            k_hot = jnp.where(k_iota == index >> 6, 1.0, 0.0)
            j_at = (index & 63) + lane_block * BLOCK
            j_hot = jnp.where(j_iota == j_at, 1.0, 0.0).astype(BF16)
            mask = dot(k_hot.astype(BF16), j_hot, NT)
            picked = dot(coef.astype(BF16), j_hot)
            rows.append(jnp.sum(picked * k_hot, axis=0, keepdims=True))
            masked.append(coef * mask)
        fields = two_sided(masked, *inverse)
        for i, row, old, field in zip(tiles, rows, fresh, fields):
            store(i, (old - field).astype(BF16), row)
        return carry

    lax.fori_loop(0, count // unroll, body, 0)


def tile_at(start):
    return pl.ds(pl.multiple_of(start, TILE), TILE)


def encode_own(momentum_ref, grad_ref, index_ref, *refs):
    table_refs, (out_ref, kept_ref) = refs[:6], refs[6:]
    columns = grad_ref.shape[1]
    count = columns // TILE
    first = lax.axis_index("section") * count

    def store(i, value, row):
        out_ref[:, tile_at(i * TILE)] = value
        kept_ref[pl.ds(i, 1), :] = row

    encode_tiles(
        count, first, lambda i: momentum_ref[:, tile_at((first + i) * TILE)],
        lambda i: grad_ref[:, tile_at(i * TILE)], index_ref, table_refs, store,
    )


def encode_rest(sections, momentum_ref, own_ref, own_kept_ref, index_ref, *refs):
    grad_refs, refs = refs[: sections - 1], refs[sections - 1 :]
    table_refs, (out_ref, kept_ref) = refs[:6], refs[6:]
    columns = own_ref.shape[1]
    count = columns // TILE
    me = lax.axis_index("section")

    def copy(i, carry):
        out_ref[:, tile_at((me * count + i) * TILE)] = own_ref[:, tile_at(i * TILE)]
        kept_ref[pl.ds(me * count + i, 1), :] = own_kept_ref[pl.ds(i, 1), :]
        return carry

    lax.fori_loop(0, count, copy, 0)
    for step, grad_ref in enumerate(grad_refs, 1):
        first = lax.rem(me + sections - step, sections) * count

        def store(i, value, row, first=first):
            out_ref[:, tile_at((first + i) * TILE)] = value
            kept_ref[pl.ds(first + i, 1), :] = row

        encode_tiles(
            count, first, lambda i: momentum_ref[:, tile_at((first + i) * TILE)],
            lambda i: grad_ref[:, tile_at(i * TILE)], index_ref, table_refs, store,
        )


def decode_kernel(kept_ref, k_ref, j_ref, il, irh, irl, out_ref):
    columns = out_ref.shape[1]
    per = TILE // BLOCK
    entries = k_ref.shape[2]
    inverse = (il[...], irh[...], irl[...])
    iota = lax.broadcasted_iota(jnp.int32, (BLOCK, entries), 0).astype(F32).astype(BF16)
    zero, one = jnp.zeros((), BF16), jnp.ones((), BF16)
    unroll = math.gcd(4, columns // TILE)

    def body(n, carry):
        sums = []
        for u in range(unroll):
            i = n * unroll + u
            ks, js, values = k_ref[i], j_ref[i], kept_ref[i]
            blocks = []
            for b in range(per):
                k_hot = jnp.where(iota == ks[b : b + 1, :], values[b : b + 1, :], zero)
                j_hot = jnp.where(iota == js[b : b + 1, :], one, zero)
                blocks.append(dot(k_hot, j_hot, NT))
            sums.append(jnp.concatenate(blocks, axis=1))
        for u, field in enumerate(two_sided(sums, *inverse)):
            out_ref[:, tile_at((n * unroll + u) * TILE)] = field.astype(BF16)
        return carry

    lax.fori_loop(0, columns // TILE // unroll, body, 0)


MESH = pl.DeviceIdType.MESH


def gather_kernel(value_ref, out_ref, send_sem, recv_sem):
    count = out_ref.shape[0]
    me = lax.axis_index("dp")
    section = lax.axis_index("section")
    barrier = pltpu.get_barrier_semaphore()
    peers = [lax.rem(me + k, count) for k in range(1, count)]
    for peer in peers:
        pl.semaphore_signal(barrier, inc=1, device_id=(section, peer), device_id_type=MESH)
    pl.semaphore_wait(barrier, count - 1)
    copies = []
    for k, peer in enumerate(peers):
        copies.append(
            pltpu.make_async_remote_copy(
                src_ref=value_ref, dst_ref=out_ref.at[me],
                send_sem=send_sem.at[k], recv_sem=recv_sem.at[k],
                device_id=(section, peer), device_id_type=MESH,
            )
        )
        copies[-1].start()
    out_ref[me] = value_ref[...]
    for copy in copies:
        copy.wait()


def gather(value, collective_id):
    count = lax.axis_size("dp")
    return pl.pallas_call(
        gather_kernel,
        out_shape=jax.ShapeDtypeStruct((count,) + value.shape, value.dtype),
        in_specs=[VMEM],
        out_specs=VMEM,
        scratch_shapes=[pltpu.SemaphoreType.DMA((count - 1,)), pltpu.SemaphoreType.DMA((count - 1,))],
        compiler_params=pltpu.CompilerParams(collective_id=collective_id, has_side_effects=True),
    )(value)


def window_kernel(sections, weight_ref, index_ref, out_ref, index_out, local_sem, send_sem, recv_sem,
                  pass_send, pass_recv, index_send, index_recv):
    count = index_out.shape[0]
    half = out_ref.shape[2] // 2
    columns = 2 * half
    me, section = lax.axis_index("dp"), lax.axis_index("section")
    twin = me + 1 - 2 * lax.rem(me, 2)
    mine = lax.rem(me, 2)
    others = [lax.rem(section + k, sections) for k in range(1, sections)]
    peers = [lax.rem(me + k, count) for k in range(1, count)]
    barrier = pltpu.get_barrier_semaphore()
    for other in others:
        pl.semaphore_signal(barrier, inc=1, device_id=(other, me), device_id_type=MESH)
    for peer in peers:
        pl.semaphore_signal(barrier, inc=1, device_id=(section, peer), device_id_type=MESH)
    pl.semaphore_wait(barrier, sections + count - 2)
    my_half = pl.ds(pl.multiple_of(mine * half, half), half)
    sends = []
    for k, other in enumerate(others):
        source = pl.ds(pl.multiple_of(other * columns + mine * half, half), half)
        sends.append(
            pltpu.make_async_remote_copy(
                src_ref=weight_ref.at[:, source], dst_ref=out_ref.at[section, :, my_half],
                send_sem=send_sem.at[k], recv_sem=recv_sem.at[k],
                device_id=(other, me), device_id_type=MESH,
            )
        )
        sends[-1].start()
    own = pltpu.make_async_copy(
        weight_ref.at[:, pl.ds(pl.multiple_of(section * columns, columns), columns)],
        out_ref.at[section], local_sem,
    )
    own.start()
    index_copies = []
    for k, peer in enumerate(peers):
        index_copies.append(
            pltpu.make_async_remote_copy(
                src_ref=index_ref, dst_ref=index_out.at[me],
                send_sem=index_send.at[k], recv_sem=index_recv.at[k],
                device_id=(section, peer), device_id_type=MESH,
            )
        )
        index_copies[-1].start()
    index_out[me] = index_ref[...]
    passes = []
    for k, send in enumerate(sends):
        send.wait_recv()
        layer = lax.rem(section + sections - 1 - k, sections)
        passes.append(
            pltpu.make_async_remote_copy(
                src_ref=out_ref.at[layer, :, my_half], dst_ref=out_ref.at[layer, :, my_half],
                send_sem=pass_send.at[k], recv_sem=pass_recv.at[k],
                device_id=(section, twin), device_id_type=MESH,
            )
        )
        passes[-1].start()
    for copy in passes + index_copies:
        copy.wait()
    for send in sends:
        send.wait_send()
    own.wait()


def windows(weight, index, sections, collective_id):
    count = lax.axis_size("dp")
    dma = pltpu.SemaphoreType.DMA
    rows, width = weight.shape
    return pl.pallas_call(
        functools.partial(window_kernel, sections),
        out_shape=(
            jax.ShapeDtypeStruct((sections, rows, width // sections), weight.dtype),
            jax.ShapeDtypeStruct((count,) + index.shape, index.dtype),
        ),
        in_specs=[VMEM, VMEM],
        out_specs=(VMEM, VMEM),
        scratch_shapes=[dma] + [dma((sections - 1,))] * 4 + [dma((count - 1,))] * 2,
        compiler_params=pltpu.CompilerParams(collective_id=collective_id, has_side_effects=True),
    )(weight, index)


def call(kernel, out_shape, *args):
    return pl.pallas_call(
        kernel,
        out_shape=out_shape,
        in_specs=[VMEM] * len(args),
        out_specs=jax.tree.map(lambda _: VMEM, out_shape),
        cost_estimate=pl.CostEstimate(flops=10**9, bytes_accessed=4 * 2**20, transcendentals=0),
    )(*args)


def shifts(axis):
    count = lax.axis_size(axis)
    for step in range(1, count):
        yield step, [(source, (source + step) % count) for source in range(count)]


def local(inputs, cotangent, weights, momentum, keep_index):
    sections = lax.axis_size("section")
    replicas = lax.axis_size("dp")
    me = lax.axis_index("section")
    rows, width = weights.shape[1:]
    columns = inputs.shape[1]
    groups, kept_count = keep_index.shape[2:]
    per = TILE // BLOCK
    tiles = groups // per
    index = keep_index[0, 0].reshape(tiles, per * kept_count)

    def by_block(value):
        value = value.reshape(replicas, groups, kept_count).transpose(1, 0, 2)
        return value.reshape(tiles, per, replicas * kept_count)

    window, index_all = windows(weights[0], index, sections, 0)
    window = window.reshape(sections * rows, columns)
    stack = jnp.concatenate([inputs, cotangent, window], axis=0)
    sums = lax.dot_general(stack, window, NT, preferred_element_type=F32)
    total = sums
    for _, pairs in shifts("section"):
        total = total + lax.ppermute(sums, "section", pairs)

    grads = call(
        functools.partial(grads_kernel, sections),
        jax.ShapeDtypeStruct((sections * rows, columns), BF16),
        total, inputs, cotangent, window,
    ).reshape(sections, rows, columns)

    def grad_of(i):
        return lax.dynamic_index_in_dim(grads, i, 0, keepdims=False)

    received = [
        lax.ppermute(grad_of((me + step) % sections), "section", pairs)
        for step, pairs in shifts("section")
    ]
    inverse = tables(True)
    every = tables(False) + inverse
    own_tiles = columns // TILE
    own_out, own_kept = call(
        encode_own,
        (
            jax.ShapeDtypeStruct((rows, columns), BF16),
            jax.ShapeDtypeStruct((own_tiles, per * kept_count), F32),
        ),
        momentum[0, 0], grad_of(me), index, *every,
    )
    index_all = by_block(index_all)
    k_all = (index_all >> 6).astype(F32).astype(BF16)
    j_all = (index_all & 63).astype(F32).astype(BF16)
    momentum_out, kept = call(
        functools.partial(encode_rest, sections),
        (
            jax.ShapeDtypeStruct((rows, width), BF16),
            jax.ShapeDtypeStruct((tiles, per * kept_count), F32),
        ),
        momentum[0, 0], own_out, own_kept, index, *received, *every,
    )
    kept_all = by_block(gather(kept.astype(BF16), 1))
    update = call(
        decode_kernel,
        jax.ShapeDtypeStruct((rows, width), BF16),
        kept_all, k_all, j_all, *inverse,
    )
    return momentum_out[None, None], update[None, None]


def solution(mesh):
    return jax.shard_map(
        local,
        mesh=mesh,
        in_specs=(
            P("dp", "section"),
            P("dp", "section"),
            P("section", None, None),
            P("section", "dp", None, None),
            P("section", "dp", None, None),
        ),
        out_specs=(P("section", "dp", None, None), P("section", "dp", None, None)),
        check_vma=False,
    )
```

time: 134 us -> 81.3 us (0.61)
  blocking collectives: 40.1 us -> 0 us
  waiting for transfers between devices: 16.1 us -> 10.2 us
  starting transfers between devices: 6.36 us -> 1.15 us
  Pallas kernels: 55.7 us -> 53.6 us
  matrix products: 1.01 us -> 2.84 us
    all_gather x2 -> x0, blocking collectives: 40.1 us -> none  [the longest x1 22.3 us: local(): index_all = lax.all_gather(keep_index[0, 0], 'dp')]
    pallas_call x3 -> x4, Pallas kernels: 55.7 us -> 27.5 us  [call(): pl.pallas_call(kernel, out_shape=out_shape, in_specs=[VMEM] * len(args),...]
    pallas_call x0 -> x2, Pallas kernels: none -> 26.1 us  [the longest x1 17.9 us: windows(): pl.pallas_call(functools.partial(window_kernel, sections), out_shape=(jax...]
    ppermute x2 -> x1, waiting for transfers between devices: 11.8 us -> 3.57 us  [local(): lax.ppermute(grad_of((me + step) % sections), 'section', pairs)]
    ppermute x2 -> x1, starting transfers between devices: 4.56 us -> 0.55 us  [local(): lax.ppermute(grad_of((me + step) % sections), 'section', pairs)]
    broadcast_in_dim x7 -> x0, local copies, waits for them, and re-layouts: 3.57 us -> none  [the longest x2 2.28 us: exchange(): stacked = jnp.broadcast_to(own[None], (count,) + own.shape)]
    convert_element_type x0 -> x6, local copies, waits for them, and re-layouts: none -> 3.24 us  [the longest x3 1.62 us: local(): j_all = (index_all & 63).astype(F32).astype(BF16)]
    ppermute x1, waiting for transfers between devices: 4.33 us -> 6.64 us  [local(): total = total + lax.ppermute(sums, 'section', pairs)]
  transfers between devices with their start and end apart: 3 -> 2, of which waited for: 2 -> 2; matrix products, arithmetic and copies ran while one was open for 3% -> 4% of each run, Pallas kernels for 0% -> 7%
where the time goes in v2:
time: 81.3 us; the launch traced here: 80.9 us
  Pallas kernels  53.6 us (66%)
  local copies, waits for them, and re-layouts  10.3 us (13%)
  waiting for transfers between devices  10.2 us (13%)
  matrix products  2.84 us (3%)
  other arithmetic  2.07 us (3%)
  starting transfers between devices  1.15 us (1%)
    pallas_call x4, Pallas kernels, call(): pl.pallas_call(kernel, out_shape=out_shape, in_specs=[VMEM] * len(args),...  27.5 us
    pallas_call x1, Pallas kernels, windows(): pl.pallas_call(functools.partial(window_kernel, sections), out_shape=(jax...  17.9 us
    pallas_call x1, Pallas kernels, gather(): pl.pallas_call(gather_kernel, out_shape=jax.ShapeDtypeStruct((count,) + v...  8.19 us
    ppermute x1, waiting for transfers between devices, local(): total = total + lax.ppermute(sums, 'section', pairs)  6.64 us
    ppermute x1, waiting for transfers between devices, local(): lax.ppermute(grad_of((me + step) % sections), 'section', pairs)  3.57 us
    dot_general x1, matrix products, local(): sums = lax.dot_general(stack, window, NT, preferred_element_type=F32)  2.84 us
    squeeze x1, local copies, waits for them, and re-layouts, grad_of(): return lax.dynamic_index_in_dim(grads, i, 0, keepdims=False)  2.12 us
    unnamed x7, local copies, waits for them, and re-layouts  1.71 us
  transfers between devices with their start and end apart: 2, of which 2 were waited for; matrix products, arithmetic and copies ran while one was open for 4% of the time, Pallas kernels for 7%

profile of v2, /device:TPU:0, one launch (start us, length us, event | category | flops | bytes accessed | tf_op | source)
XLA Modules:
  0.0 80.9 jit_solution(10564713714824465124)
XLA Ops:
  0.6 0.0 copy-start
  0.6 0.9 %copy.17 = s32[1,1,128,32]{3,2,1,0:T(8,128)S(1)} copy(s32[1,1,128,32]{2,3,1,0:T(8,128)} %param.15) | data formatting | bytes 32768 | tf_op args[4]
  1.5 0.7 reshape_squeeze.3.index_ref
  2.2 17.9 %shard_map.122 = (bf16[2,64,4096]{2,1,0:T(8,128)(2,1)}, s32[16,32,128]{2,1,0:T(8,128)}) custom-call(bf16[64,8192]{1,0:T(8,128)(2,1)} %bitcast.20, s32[32,128]{1,0:T(8,128)} %reshape_squeeze.3.index_ref), custom_call_target="tpu_custom_call" | custom-call | tf_op jit(solution)/shard_map/pallas_call | solution.py:338
  20.2 0.0 copy-done
  20.2 2.8 %fusion = f32[384,128]{1,0:T(8,128)S(1)} fusion(bf16[128,4096]{1,0:T(8,128)(2,1)} %bitcast.21, bf16[128,4096]{1,0:T(8,128)(2,1)S(1)} %copy-done, bf16[128,4096]{1,0:T(8,128)(2,1)} %x_ref.1), kind=kOutput, calls=%fused_computation | convolution fusion | flops 412090368 | bytes 3342336 | tf_op jit(solution)/shard_map/dot_general | solution.py:385
  23.0 0.6 collective-permute-start
  23.6 6.6 %collective-permute-done = f32[384,128]{1,0:T(8,128)S(1)} collective-permute-done((f32[384,128]{1,0:T(8,128)S(1)}, f32[384,128]{1,0:T(8,128)S(1)}, u32[]{:S(2)}, u32[]{:S(2)}) %collective-permute-start) | collective-permute-done | bytes 196640 | tf_op jit(solution)/shard_map/ppermute | solution.py:388
  30.3 0.7 add.17.sums_ref
  31.0 5.5 %shard_map.123 = bf16[128,4096]{1,0:T(8,128)(2,1)} custom-call(f32[384,128]{1,0:T(8,128)} %add.17.sums_ref, bf16[128,4096]{1,0:T(8,128)(2,1)} %x_ref.1, bf16[128,4096]{1,0:T(8,128)(2,1)} %g_ref.1, bf16[128,4096]{1,0:T(8,128)(2,1)} %bitcast.22), custom_call_target="tpu_custom_call" | custom-call | flops 1000000000 | bytes 4194304 | tf_op jit(solution)/shard_map/pallas_call | solution.py:352
  36.4 0.0 copy-start.1
  36.4 2.1 %dynamic-slice_bitcast_fusion = (bf16[64,4096]{1,0:T(8,128)(2,1)S(1)}, bf16[64,4096]{1,0:T(8,128)(2,1)}) fusion(bf16[2,64,4096]{2,1,0:T(8,128)(2,1)} %bitcast.16, s32[]{:T(128)S(6)} %select_n.16, s32[]{:T(128)S(6)} %select_n.14), kind=kLoop, calls=%fused_computation.6 | loop fusion | bytes 2097160 | tf_op jit(solution)/shard_map/jit(dynamic_index_in_dim)/squeeze | solution.py:397
  38.6 0.5 collective-permute-start.1
  39.1 0.0 copy-done.1
  39.1 0.1 convert_convert_fusion
  39.2 0.2 convert_element_type.31
  39.4 0.3 copy.19
  39.8 1.0 %convert_element_type.33.k_ref = bf16[32,4,512]{2,1,0:T(4,128)(2,1)} reshape(bf16[128,16,32]{2,1,0:T(8,128)(2,1)S(1)} %copy.19) | data formatting | bytes 262144 | tf_op jit(solution)/shard_map/convert_element_type | solution.py:415
  40.8 0.2 convert_element_type.35
  41.0 0.3 copy.20
  41.4 1.0 %convert_element_type.37.j_ref = bf16[32,4,512]{2,1,0:T(4,128)(2,1)} reshape(bf16[128,16,32]{2,1,0:T(8,128)(2,1)S(1)} %copy.20) | data formatting | bytes 262144 | tf_op jit(solution)/shard_map/convert_element_type | solution.py:416
  42.4 5.9 %shard_map.124 = (bf16[64,4096]{1,0:T(8,128)(2,1)}, f32[16,128]{1,0:T(8,128)}) custom-call(bf16[64,8192]{1,0:T(8,128)(2,1)} %bitcast.23, bf16[64,4096]{1,0:T(8,128)(2,1)} %get-tuple-element.15.grad_ref, s32[32,128]{1,0:T(8,128)} %reshape_squeeze.3.index_ref, bf16[64,192]{1,0:T(8,128)(2,1)} %constant.45.clone.refs_0_.refs_1_, ...), custom_call_target="tpu_custom_call" | custom-call | flops 1000000000 | bytes 4194304 | tf_op jit(solution)/shard_map/pallas_call | solution.py:352
  48.3 3.6 %collective-permute-done.1.refs_0_ = bf16[64,4096]{1,0:T(8,128)(2,1)S(1)} collective-permute-done((bf16[64,4096]{1,0:T(8,128)(2,1)S(1)}, bf16[64,4096]{1,0:T(8,128)(2,1)S(1)}, u32[]{:S(2)}, u32[]{:S(2)}) %collective-permute-start.1) | collective-permute-done | bytes 524320 | tf_op jit(solution)/shard_map/ppermute | solution.py:400
  51.9 0.0 copy-start.2
  51.9 0.8 copy-done.2
  52.7 6.4 %shard_map.125 = (bf16[64,8192]{1,0:T(8,128)(2,1)}, f32[32,128]{1,0:T(8,128)}) custom-call(bf16[64,8192]{1,0:T(8,128)(2,1)} %bitcast.24, bf16[64,4096]{1,0:T(8,128)(2,1)} %get-tuple-element.9.own_ref, f32[16,128]{1,0:T(8,128)} %get-tuple-element.10.own_kept_ref, s32[32,128]{1,0:T(8,128)} %reshape_squeeze.3.index_ref, bf16[64,4096]{1,0:T(8,128)(2,1)} %copy-done.2, ...), custom_call_target="tpu_custom_call" | custom-call | flops 1000000000 | bytes 4194304 | tf_op jit(solution)/shard_map/pallas_call | solution.py:352
  59.1 1.3 %convert_element_type.29.value_ref = bf16[32,128]{1,0:T(8,128)(2,1)} convert(f32[32,128]{1,0:T(8,128)} %get-tuple-element.12) | non-fusion elementwise | flops 4096 | bytes 24576 | tf_op jit(solution)/shard_map/convert_element_type | solution.py:425
  60.4 8.2 %shard_map.126 = bf16[16,32,128]{2,1,0:T(8,128)(2,1)} custom-call(bf16[32,128]{1,0:T(8,128)(2,1)} %convert_element_type.29.value_ref), custom_call_target="tpu_custom_call" | custom-call | tf_op jit(solution)/shard_map/pallas_call | solution.py:261
  68.6 1.1 %reshape.36 = bf16[16,128,32]{2,1,0:T(8,128)(2,1)S(1)} reshape(bf16[16,32,128]{2,1,0:T(8,128)(2,1)} %shard_map.126) | data formatting | bytes 262144 | tf_op jit(solution)/shard_map/reshape | solution.py:379
  69.7 0.3 copy.18
  70.1 1.0 %reshape.37.kept_ref = bf16[32,4,512]{2,1,0:T(4,128)(2,1)} reshape(bf16[128,16,32]{2,1,0:T(8,128)(2,1)S(1)} %copy.18) | data formatting | bytes 262144 | tf_op jit(solution)/shard_map/reshape | solution.py:380
  71.1 9.7 %shard_map.127 = bf16[64,8192]{1,0:T(8,128)(2,1)} custom-call(bf16[32,4,512]{2,1,0:T(4,128)(2,1)} %reshape.37.kept_ref, bf16[32,4,512]{2,1,0:T(4,128)(2,1)} %convert_element_type.33.k_ref, bf16[32,4,512]{2,1,0:T(4,128)(2,1)} %convert_element_type.37.j_ref, bf16[64,192]{1,0:T(8,128)(2,1)} %constant.42.clone.refs_3_.refs_4_.il, ...), custom_call_target="tpu_custom_call" | custom-call | flops 1000000000 | bytes 4194304 | tf_op jit(solution)/shard_map/pallas_call | solution.py:352
Async XLA Ops:
  0.6 19.5 %copy-start = (bf16[128,4096]{1,0:T(8,128)(2,1)S(1)}, bf16[128,4096]{1,0:T(8,128)(2,1)}, u32[]{:S(2)}) copy-start(bf16[128,4096]{1,0:T(8,128)(2,1)} %g_ref.1) | copy-start | bytes 3145732
  23.0 7.2 %collective-permute-start = (f32[384,128]{1,0:T(8,128)S(1)}, f32[384,128]{1,0:T(8,128)S(1)}, u32[]{:S(2)}, u32[]{:S(2)}) collective-permute-start(f32[384,128]{1,0:T(8,128)S(1)} %fusion), channel_id=1, source_target_pairs={{0,16},{16,0},{1,17},{17,1},{2,18},{18,2},{3,19},{19,3},{4,20},{20... | collective-permute-start | bytes 589832 | tf_op jit(solution)/shard_map/ppermute | solution.py:388
  36.4 2.7 %copy-start.1 = (s32[16,32,128]{2,1,0:T(8,128)S(1)}, s32[16,32,128]{2,1,0:T(8,128)}, u32[]{:S(2)}) copy-start(s32[16,32,128]{2,1,0:T(8,128)} %get-tuple-element.13) | copy-start | bytes 786436
  38.6 13.3 %collective-permute-start.1 = (bf16[64,4096]{1,0:T(8,128)(2,1)S(1)}, bf16[64,4096]{1,0:T(8,128)(2,1)S(1)}, u32[]{:S(2)}, u32[]{:S(2)}) collective-permute-start(bf16[64,4096]{1,0:T(8,128)(2,1)S(1)} %get-tuple-element.14), channel_id=1, source_target_pairs={{0,16},{16,0},{1,17},{17,1},{2,18},{18,2},{3,19},{19,3},{4,20},{20... | collective-permute-start | bytes 1572872 | tf_op jit(solution)/shard_map/ppermute | solution.py:400
  51.9 0.8 copy-start.2

commit v3 on v2

--- a/solution.py
+++ b/solution.py
@@ -78,10 +78,11 @@
     return v / (1.0 + jnp.exp(-v))
 
 
-def grads_kernel(layers, sums_ref, x_ref, g_ref, w_ref, out_ref):
+def grads_kernel(layers, sums_ref, got_ref, x_ref, g_ref, w_ref, *refs):
+    out_refs, lhs_ref = refs[:layers], refs[layers]
     tokens, columns = x_ref.shape
     rows = w_ref.shape[0] // layers
-    sums = sums_ref[...]
+    sums = sums_ref[...] + got_ref[...].astype(F32)
 
     def of(base, count, layer):
         return sums[base : base + count, layer * rows : (layer + 1) * rows]
@@ -111,6 +112,15 @@
     cross = jnp.where(col > row, a_d, jnp.where(col < row, d_a, 0.0))
     cross_high, cross_low = split(cross)
 
+    factors = jnp.concatenate([a_t, d_t, cross_high, cross_low], axis=1)
+    for l in range(layers):
+        lhs_ref[l] = factors[l * rows : (l + 1) * rows]
+    me = lax.axis_index("section")
+    turned = [lhs_ref[lax.rem(me + k, layers)] for k in range(layers)]
+    factors = jnp.concatenate(turned, axis=0)
+    a_t, d_t = factors[:, :tokens], factors[:, tokens : 2 * tokens]
+    cross_high = factors[:, 2 * tokens : 2 * tokens + layers * rows]
+    cross_low = factors[:, 2 * tokens + layers * rows :]
     step = math.gcd(4 * TILE, columns)
 
     def body(i, carry):
@@ -118,7 +128,8 @@
         w = w_ref[:, at]
         total = dot(a_t, g_ref[:, at]) + dot(d_t, x_ref[:, at])
         total = total + dot(cross_high, w) + dot(cross_low, w)
-        out_ref[:, at] = total.astype(BF16)
+        for k, out_ref in enumerate(out_refs):
+            out_ref[:, at] = total[k * rows : (k + 1) * rows].astype(BF16)
         return carry
 
     lax.fori_loop(0, columns // step, body, 0)
@@ -129,7 +140,8 @@
     entries = index_ref.shape[1]
     forward = [ref[...] for ref in table_refs[:3]]
     inverse = [ref[...] for ref in table_refs[3:]]
-    lane_block = lax.broadcasted_iota(jnp.int32, (1, entries), 1) // (entries // per)
+    slot = lax.broadcasted_iota(jnp.int32, (1, entries), 1) // (entries // per)
+    lane_block = (slot + per - lax.rem(lax.axis_index("dp"), per)) & (per - 1)
     k_iota = lax.broadcasted_iota(jnp.int32, (BLOCK, entries), 0)
     j_iota = lax.broadcasted_iota(jnp.int32, (TILE, entries), 0)
     unroll = math.gcd(8, count)
@@ -178,7 +190,7 @@
 
 def encode_rest(sections, momentum_ref, own_ref, own_kept_ref, index_ref, *refs):
     grad_refs, refs = refs[: sections - 1], refs[sections - 1 :]
-    table_refs, (out_ref, kept_ref) = refs[:6], refs[6:]
+    table_refs, (out_ref, rounded_ref, kept_ref) = refs[:6], refs[6:]
     columns = own_ref.shape[1]
     count = columns // TILE
     me = lax.axis_index("section")
@@ -200,26 +212,42 @@
             count, first, lambda i: momentum_ref[:, tile_at((first + i) * TILE)],
             lambda i: grad_ref[:, tile_at(i * TILE)], index_ref, table_refs, store,
         )
-
-
-def decode_kernel(kept_ref, k_ref, j_ref, il, irh, irl, out_ref):
+    rounded_ref[...] = kept_ref[...].astype(BF16)
+
+
+def decode_kernel(kept_ref, index_ref, il, irh, irl, out_ref):
     columns = out_ref.shape[1]
     per = TILE // BLOCK
-    entries = k_ref.shape[2]
+    replicas, _, lanes = index_ref.shape
+    entries = replicas // per * lanes
     inverse = (il[...], irh[...], irl[...])
     iota = lax.broadcasted_iota(jnp.int32, (BLOCK, entries), 0).astype(F32).astype(BF16)
     zero, one = jnp.zeros((), BF16), jnp.ones((), BF16)
+    slot = lax.broadcasted_iota(jnp.int32, (1, lanes), 1) // (lanes // per)
     unroll = math.gcd(4, columns // TILE)
+
+    def merged(rows, b):
+        parts = []
+        for q in range(0, replicas, per):
+            part = rows[q]
+            for p in range(1, per):
+                part = jnp.where(slot == (b + p) % per, rows[q + p], part)
+            parts.append(part)
+        return jnp.concatenate(parts, axis=1)
 
     def body(n, carry):
         sums = []
         for u in range(unroll):
             i = n * unroll + u
-            ks, js, values = k_ref[i], j_ref[i], kept_ref[i]
+            values = [kept_ref[q, pl.ds(i, 1), :] for q in range(replicas)]
+            indices = [index_ref[q, pl.ds(i, 1), :] for q in range(replicas)]
             blocks = []
             for b in range(per):
-                k_hot = jnp.where(iota == ks[b : b + 1, :], values[b : b + 1, :], zero)
-                j_hot = jnp.where(iota == js[b : b + 1, :], one, zero)
+                index = merged(indices, b)
+                k_row = (index >> 6).astype(F32).astype(BF16)
+                j_row = (index & 63).astype(F32).astype(BF16)
+                k_hot = jnp.where(iota == k_row, merged(values, b).astype(BF16), zero)
+                j_hot = jnp.where(iota == j_row, one, zero)
                 blocks.append(dot(k_hot, j_hot, NT))
             sums.append(jnp.concatenate(blocks, axis=1))
         for u, field in enumerate(two_sided(sums, *inverse)):
@@ -232,17 +260,25 @@
 MESH = pl.DeviceIdType.MESH
 
 
-def gather_kernel(value_ref, out_ref, send_sem, recv_sem):
-    count = out_ref.shape[0]
+def inner_of(count):
+    return math.gcd(4, count)
+
+
+def neighbours(count):
+    inner = inner_of(count)
     me = lax.axis_index("dp")
+    place = lax.rem(me, inner)
+    base = me - place
+    near = [base + lax.rem(place + k, inner) for k in range(1, inner)]
+    far = [lax.rem(me + k * inner, count) for k in range(1, count // inner)]
+    return me, base, near, far
+
+
+def gather_near(value_ref, out_ref, send_sem, recv_sem):
+    me, _, near, _ = neighbours(out_ref.shape[0])
     section = lax.axis_index("section")
-    barrier = pltpu.get_barrier_semaphore()
-    peers = [lax.rem(me + k, count) for k in range(1, count)]
-    for peer in peers:
-        pl.semaphore_signal(barrier, inc=1, device_id=(section, peer), device_id_type=MESH)
-    pl.semaphore_wait(barrier, count - 1)
     copies = []
-    for k, peer in enumerate(peers):
+    for k, peer in enumerate(near):
         copies.append(
             pltpu.make_async_remote_copy(
                 src_ref=value_ref, dst_ref=out_ref.at[me],
@@ -251,80 +287,120 @@
             )
         )
         copies[-1].start()
-    out_ref[me] = value_ref[...]
+    return copies
+
+
+def gather_far(out_ref, send_sem, recv_sem):
+    _, base, near, far = neighbours(out_ref.shape[0])
+    section = lax.axis_index("section")
+    group = out_ref.at[pl.ds(base, len(near) + 1)]
+    copies = []
+    for k, peer in enumerate(far):
+        copies.append(
+            pltpu.make_async_remote_copy(
+                src_ref=group, dst_ref=group,
+                send_sem=send_sem.at[len(near) + k], recv_sem=recv_sem.at[len(near) + k],
+                device_id=(section, peer), device_id_type=MESH,
+            )
+        )
+        copies[-1].start()
+    return copies
+
+
+def gather_count(count):
+    inner = inner_of(count)
+    return inner - 1 + count // inner - 1
+
+
+def gather_kernel(value_ref, out_ref, own_sem, send_sem, recv_sem):
+    me, _, near, far = neighbours(out_ref.shape[0])
+    section = lax.axis_index("section")
+    barrier = pltpu.get_barrier_semaphore()
+    for peer in near + far:
+        pl.semaphore_signal(barrier, inc=1, device_id=(section, peer), device_id_type=MESH)
+    own = pltpu.make_async_copy(value_ref, out_ref.at[me], own_sem)
+    own.start()
+    pl.semaphore_wait(barrier, len(near) + len(far))
+    copies = gather_near(value_ref, out_ref, send_sem, recv_sem)
+    own.wait()
     for copy in copies:
         copy.wait()
+    for copy in gather_far(out_ref, send_sem, recv_sem):
+        copy.wait()
 
 
 def gather(value, collective_id):
     count = lax.axis_size("dp")
+    dma = pltpu.SemaphoreType.DMA
     return pl.pallas_call(
         gather_kernel,
         out_shape=jax.ShapeDtypeStruct((count,) + value.shape, value.dtype),
         in_specs=[VMEM],
         out_specs=VMEM,
-        scratch_shapes=[pltpu.SemaphoreType.DMA((count - 1,)), pltpu.SemaphoreType.DMA((count - 1,))],
+        scratch_shapes=[dma] + [dma((gather_count(count),))] * 2,
         compiler_params=pltpu.CompilerParams(collective_id=collective_id, has_side_effects=True),
     )(value)
 
 
-def window_kernel(sections, weight_ref, index_ref, out_ref, index_out, local_sem, send_sem, recv_sem,
+CHUNKS = 2
+
+
+def window_kernel(sections, weight_ref, index_ref, out_ref, index_out, local_sem, own_sem, send_sem, recv_sem,
                   pass_send, pass_recv, index_send, index_recv):
-    count = index_out.shape[0]
     half = out_ref.shape[2] // 2
     columns = 2 * half
-    me, section = lax.axis_index("dp"), lax.axis_index("section")
+    piece = out_ref.shape[1] // CHUNKS
+    me, _, near, far = neighbours(index_out.shape[0])
+    section = lax.axis_index("section")
     twin = me + 1 - 2 * lax.rem(me, 2)
     mine = lax.rem(me, 2)
     others = [lax.rem(section + k, sections) for k in range(1, sections)]
-    peers = [lax.rem(me + k, count) for k in range(1, count)]
     barrier = pltpu.get_barrier_semaphore()
     for other in others:
         pl.semaphore_signal(barrier, inc=1, device_id=(other, me), device_id_type=MESH)
-    for peer in peers:
+    for peer in near + far:
         pl.semaphore_signal(barrier, inc=1, device_id=(section, peer), device_id_type=MESH)
-    pl.semaphore_wait(barrier, sections + count - 2)
-    my_half = pl.ds(pl.multiple_of(mine * half, half), half)
-    sends = []
-    for k, other in enumerate(others):
-        source = pl.ds(pl.multiple_of(other * columns + mine * half, half), half)
-        sends.append(
-            pltpu.make_async_remote_copy(
-                src_ref=weight_ref.at[:, source], dst_ref=out_ref.at[section, :, my_half],
-                send_sem=send_sem.at[k], recv_sem=recv_sem.at[k],
-                device_id=(other, me), device_id_type=MESH,
-            )
-        )
-        sends[-1].start()
     own = pltpu.make_async_copy(
         weight_ref.at[:, pl.ds(pl.multiple_of(section * columns, columns), columns)],
         out_ref.at[section], local_sem,
     )
     own.start()
-    index_copies = []
-    for k, peer in enumerate(peers):
-        index_copies.append(
+    own_index = pltpu.make_async_copy(index_ref, index_out.at[me], own_sem)
+    own_index.start()
+    pl.semaphore_wait(barrier, len(others) + len(near) + len(far))
+    my_half = pl.ds(pl.multiple_of(mine * half, half), half)
+    sends = []
+    for c in range(CHUNKS):
+        lines = pl.ds(c * piece, piece)
+        for k, other in enumerate(others):
+            source = pl.ds(pl.multiple_of(other * columns + mine * half, half), half)
+            sends.append(
+                pltpu.make_async_remote_copy(
+                    src_ref=weight_ref.at[lines, source], dst_ref=out_ref.at[section, lines, my_half],
+                    send_sem=send_sem.at[len(sends)], recv_sem=recv_sem.at[len(sends)],
+                    device_id=(other, me), device_id_type=MESH,
+                )
+            )
+            sends[-1].start()
+    index_copies = gather_near(index_ref, index_out, index_send, index_recv)
+    own_index.wait()
+    for copy in index_copies:
+        copy.wait()
+    waiting = gather_far(index_out, index_send, index_recv)
+    for n, send in enumerate(sends):
+        send.wait_recv()
+        layer = lax.rem(section + sections - 1 - n % (sections - 1), sections)
+        lines = pl.ds(n // (sections - 1) * piece, piece)
+        half_ref = out_ref.at[layer, lines, my_half]
+        waiting.append(
             pltpu.make_async_remote_copy(
-                src_ref=index_ref, dst_ref=index_out.at[me],
-                send_sem=index_send.at[k], recv_sem=index_recv.at[k],
-                device_id=(section, peer), device_id_type=MESH,
-            )
-        )
-        index_copies[-1].start()
-    index_out[me] = index_ref[...]
-    passes = []
-    for k, send in enumerate(sends):
-        send.wait_recv()
-        layer = lax.rem(section + sections - 1 - k, sections)
-        passes.append(
-            pltpu.make_async_remote_copy(
-                src_ref=out_ref.at[layer, :, my_half], dst_ref=out_ref.at[layer, :, my_half],
-                send_sem=pass_send.at[k], recv_sem=pass_recv.at[k],
+                src_ref=half_ref, dst_ref=half_ref,
+                send_sem=pass_send.at[n], recv_sem=pass_recv.at[n],
                 device_id=(section, twin), device_id_type=MESH,
             )
         )
-        passes[-1].start()
-    for copy in passes + index_copies:
+        waiting[-1].start()
+    for copy in waiting:
         copy.wait()
     for send in sends:
         send.wait_send()
@@ -343,17 +419,18 @@
         ),
         in_specs=[VMEM, VMEM],
         out_specs=(VMEM, VMEM),
-        scratch_shapes=[dma] + [dma((sections - 1,))] * 4 + [dma((count - 1,))] * 2,
+        scratch_shapes=[dma] * 2 + [dma(((sections - 1) * CHUNKS,))] * 4 + [dma((gather_count(count),))] * 2,
         compiler_params=pltpu.CompilerParams(collective_id=collective_id, has_side_effects=True),
     )(weight, index)
 
 
-def call(kernel, out_shape, *args):
+def call(kernel, out_shape, *args, scratch=()):
     return pl.pallas_call(
         kernel,
         out_shape=out_shape,
         in_specs=[VMEM] * len(args),
         out_specs=jax.tree.map(lambda _: VMEM, out_shape),
+        scratch_shapes=scratch,
         cost_estimate=pl.CostEstimate(flops=10**9, bytes_accessed=4 * 2**20, transcendentals=0),
     )(*args)
 
@@ -374,31 +451,24 @@
     per = TILE // BLOCK
     tiles = groups // per
     index = keep_index[0, 0].reshape(tiles, per * kept_count)
-
-    def by_block(value):
-        value = value.reshape(replicas, groups, kept_count).transpose(1, 0, 2)
-        return value.reshape(tiles, per, replicas * kept_count)
+    index = jnp.roll(index, lax.axis_index("dp") % per * kept_count, axis=1)
 
     window, index_all = windows(weights[0], index, sections, 0)
     window = window.reshape(sections * rows, columns)
     stack = jnp.concatenate([inputs, cotangent, window], axis=0)
     sums = lax.dot_general(stack, window, NT, preferred_element_type=F32)
-    total = sums
-    for _, pairs in shifts("section"):
-        total = total + lax.ppermute(sums, "section", pairs)
-
+    rounded = sums.astype(BF16)
+    got = [lax.ppermute(rounded, "section", pairs) for _, pairs in shifts("section")]
+    got = functools.reduce(jnp.add, [part.astype(F32) for part in got]) if len(got) > 1 else got[0]
+    depth = 2 * (inputs.shape[0] + sections * rows)
     grads = call(
         functools.partial(grads_kernel, sections),
-        jax.ShapeDtypeStruct((sections * rows, columns), BF16),
-        total, inputs, cotangent, window,
-    ).reshape(sections, rows, columns)
-
-    def grad_of(i):
-        return lax.dynamic_index_in_dim(grads, i, 0, keepdims=False)
-
+        [jax.ShapeDtypeStruct((rows, columns), BF16)] * sections,
+        sums, got, inputs, cotangent, window,
+        scratch=[pltpu.VMEM((sections, rows, depth), BF16)],
+    )
     received = [
-        lax.ppermute(grad_of((me + step) % sections), "section", pairs)
-        for step, pairs in shifts("section")
+        lax.ppermute(grads[step], "section", pairs) for step, pairs in shifts("section")
     ]
     inverse = tables(True)
     every = tables(False) + inverse
@@ -409,24 +479,22 @@
             jax.ShapeDtypeStruct((rows, columns), BF16),
             jax.ShapeDtypeStruct((own_tiles, per * kept_count), F32),
         ),
-        momentum[0, 0], grad_of(me), index, *every,
-    )
-    index_all = by_block(index_all)
-    k_all = (index_all >> 6).astype(F32).astype(BF16)
-    j_all = (index_all & 63).astype(F32).astype(BF16)
+        momentum[0, 0], grads[0], index, *every,
+    )
     momentum_out, kept = call(
         functools.partial(encode_rest, sections),
         (
             jax.ShapeDtypeStruct((rows, width), BF16),
-            jax.ShapeDtypeStruct((tiles, per * kept_count), F32),
+            jax.ShapeDtypeStruct((tiles, per * kept_count), BF16),
         ),
         momentum[0, 0], own_out, own_kept, index, *received, *every,
-    )
-    kept_all = by_block(gather(kept.astype(BF16), 1))
+        scratch=[pltpu.VMEM((tiles, per * kept_count), F32)],
+    )
+    kept_all = gather(kept, 1).astype(F32)
     update = call(
         decode_kernel,
         jax.ShapeDtypeStruct((rows, width), BF16),
-        kept_all, k_all, j_all, *inverse,
+        kept_all, index_all, *inverse,
     )
     return momentum_out[None, None], update[None, None]
 

time: 81.3 us -> 76.4 us (0.940)
  local copies, waits for them, and re-layouts: 10.3 us -> 2.4 us
  Pallas kernels: 53.6 us -> 55.8 us
  starting transfers between devices: 1.15 us -> 2.25 us
  waiting for transfers between devices: 10.2 us -> 9.13 us
    convert_element_type x6 -> x0, local copies, waits for them, and re-layouts: 3.24 us -> none  [the longest x3 1.62 us: local(): j_all = (index_all & 63).astype(F32).astype(BF16)]
    pallas_call x1, Pallas kernels: 8.19 us -> 10.8 us  [gather(): pl.pallas_call(gather_kernel, out_shape=jax.ShapeDtypeStruct((count,) + v...]
    reshape x2 -> x0, local copies, waits for them, and re-layouts: 2.18 us -> none  [the longest x1 1.14 us: by_block(): value = value.reshape(replicas, groups, kept_count).transpose(1, 0, 2)]
    squeeze x1 -> x0, local copies, waits for them, and re-layouts: 2.12 us -> none  [grad_of(): return lax.dynamic_index_in_dim(grads, i, 0, keepdims=False)]
    ppermute x2, starting transfers between devices: 1.15 us -> 2.25 us  [the longest x1 1.18 us: local(): lax.ppermute(grads[step], 'section', pairs)]
    ppermute x2, waiting for transfers between devices: 10.2 us -> 9.13 us  [the longest x1 5.59 us: local(): lax.ppermute(grads[step], 'section', pairs)]
  transfers between devices with their start and end apart: 2 -> 2, of which waited for: 2 -> 2; matrix products, arithmetic and copies ran while one was open for 4% -> 0% of each run, Pallas kernels for 7% -> 8%
where the time goes in v3:
time: 76.4 us; the launch traced here: 76.1 us
  Pallas kernels  55.8 us (73%)
  waiting for transfers between devices  9.13 us (12%)
  matrix products  3.5 us (5%)
  local copies, waits for them, and re-layouts  2.4 us (3%)
  other arithmetic  2.31 us (3%)
  starting transfers between devices  2.25 us (3%)
    pallas_call x4, Pallas kernels, call(): pl.pallas_call(kernel, out_shape=out_shape, in_specs=[VMEM] * len(args),...  27.8 us
    pallas_call x1, Pallas kernels, windows(): pl.pallas_call(functools.partial(window_kernel, sections), out_shape=(jax...  17.2 us
    pallas_call x1, Pallas kernels, gather(): pl.pallas_call(gather_kernel, out_shape=jax.ShapeDtypeStruct((count,) + v...  10.8 us
    ppermute x1, waiting for transfers between devices, local(): lax.ppermute(grads[step], 'section', pairs)  5.59 us
    ppermute x1, waiting for transfers between devices, local(): lax.ppermute(rounded, 'section', pairs)  3.55 us
    dot_general x1, matrix products, local(): sums = lax.dot_general(stack, window, NT, preferred_element_type=F32)  3.5 us
    unnamed x7, local copies, waits for them, and re-layouts  2.32 us
    convert_element_type x1, other arithmetic, local(): kept_all = gather(kept, 1).astype(F32)  1.63 us
  transfers between devices with their start and end apart: 2, of which 2 were waited for; matrix products, arithmetic and copies ran while one was open for 0% of the time, Pallas kernels for 8%

profile of v3, /device:TPU:0, one launch (start us, length us, event | category | flops | bytes accessed | tf_op | source)
XLA Modules:
  0.0 76.1 jit_solution(10068736471884051652)
XLA Ops:
  0.6 0.0 copy-start
  0.7 0.9 %copy.14 = s32[1,1,128,32]{3,2,1,0:T(8,128)S(1)} copy(s32[1,1,128,32]{2,3,1,0:T(8,128)} %param.15) | data formatting | bytes 32768 | tf_op args[4]
  1.6 0.1 reshape_squeeze.3
  1.6 0.7 fusion.6.index_ref
  2.3 17.2 %shard_map.122 = (bf16[2,64,4096]{2,1,0:T(8,128)(2,1)}, s32[16,32,128]{2,1,0:T(8,128)}) custom-call(bf16[64,8192]{1,0:T(8,128)(2,1)} %bitcast.8, s32[32,128]{1,0:T(8,128)} %fusion.6.index_ref), custom_call_target="tpu_custom_call" | custom-call | tf_op jit(solution)/shard_map/pallas_call | solution.py:414
  19.5 0.0 copy-done
  19.5 3.5 %fusion.8 = (bf16[384,128]{1,0:T(8,128)(2,1)S(1)}, f32[384,128]{1,0:T(8,128)}) fusion(bf16[128,4096]{1,0:T(8,128)(2,1)} %bitcast.11, bf16[128,4096]{1,0:T(8,128)(2,1)S(1)} %copy-done, bf16[128,4096]{1,0:T(8,128)(2,1)} %x_ref.1), kind=kOutput, calls=%fused_computation.10 | convolution fusion | flops 412139520 | bytes 3440640 | tf_op jit(solution)/shard_map/dot_general | solution.py:459
  23.0 1.1 %collective-permute-start = (bf16[384,128]{1,0:T(8,128)(2,1)S(1)}, bf16[384,128]{1,0:T(8,128)(2,1)S(1)}, u32[]{:S(2)}, u32[]{:S(2)}) collective-permute-start(bf16[384,128]{1,0:T(8,128)(2,1)S(1)} %get-tuple-element.18), channel_id=1, source_target_pairs={{0,16},{16,0},{1,17},{17,1},{2,18},{18,2},{3,19},{19,3},{4,20},{20... | collective-permute-start | bytes 294920 | tf_op jit(solution)/shard_map/ppermute | solution.py:461
  24.1 3.5 %collective-permute-done.got_ref = bf16[384,128]{1,0:T(8,128)(2,1)S(1)} collective-permute-done((bf16[384,128]{1,0:T(8,128)(2,1)S(1)}, bf16[384,128]{1,0:T(8,128)(2,1)S(1)}, u32[]{:S(2)}, u32[]{:S(2)}) %collective-permute-start) | collective-permute-done | bytes 98336 | tf_op jit(solution)/shard_map/ppermute | solution.py:461
  27.6 0.0 copy-start.2
  27.6 0.6 copy-done.2
  28.3 5.5 %shard_map.123 = (bf16[64,4096]{1,0:T(8,128)(2,1)}, bf16[64,4096]{1,0:T(8,128)(2,1)}) custom-call(f32[384,128]{1,0:T(8,128)} %get-tuple-element.19.sums_ref, bf16[384,128]{1,0:T(8,128)(2,1)} %copy-done.2, bf16[128,4096]{1,0:T(8,128)(2,1)} %x_ref.1, bf16[128,4096]{1,0:T(8,128)(2,1)} %g_ref.1, bf16[128,4096]{1,0:T(8,128)(2,1)} %bitcast.12), custom_call_target="tpu_custom_call" | custom-call | flops 1000000000 | bytes 4194304 | tf_op jit(solution)/shard_map/pallas_call | solution.py:428
  33.8 1.2 %collective-permute-start.1 = (bf16[64,4096]{1,0:T(8,128)(2,1)}, bf16[64,4096]{1,0:T(8,128)(2,1)S(1)}, u32[]{:S(2)}, u32[]{:S(2)}) collective-permute-start(bf16[64,4096]{1,0:T(8,128)(2,1)} %get-tuple-element.14), channel_id=1, source_target_pairs={{0,16},{16,0},{1,17},{17,1},{2,18},{18,2},{3,19},{19,3},{4,20},{20... | collective-permute-start | bytes 1572872 | tf_op jit(solution)/shard_map/ppermute | solution.py:471
  35.0 5.9 %shard_map.124 = (bf16[64,4096]{1,0:T(8,128)(2,1)}, f32[16,128]{1,0:T(8,128)}) custom-call(bf16[64,8192]{1,0:T(8,128)(2,1)} %bitcast.9, bf16[64,4096]{1,0:T(8,128)(2,1)} %get-tuple-element.11.grad_ref, s32[32,128]{1,0:T(8,128)} %fusion.6.index_ref, bf16[64,192]{1,0:T(8,128)(2,1)} %constant.55.clone.refs_0_.refs_1_, ...), custom_call_target="tpu_custom_call" | custom-call | flops 1000000000 | bytes 4194304 | tf_op jit(solution)/shard_map/pallas_call | solution.py:428
  40.9 5.6 %collective-permute-done.1.refs_0_ = bf16[64,4096]{1,0:T(8,128)(2,1)S(1)} collective-permute-done((bf16[64,4096]{1,0:T(8,128)(2,1)}, bf16[64,4096]{1,0:T(8,128)(2,1)S(1)}, u32[]{:S(2)}, u32[]{:S(2)}) %collective-permute-start.1) | collective-permute-done | bytes 524320 | tf_op jit(solution)/shard_map/ppermute | solution.py:471
  46.5 0.0 copy-start.1
  46.5 0.8 %copy-done.1 = bf16[64,4096]{1,0:T(8,128)(2,1)} copy-done((bf16[64,4096]{1,0:T(8,128)(2,1)}, bf16[64,4096]{1,0:T(8,128)(2,1)S(1)}, u32[]{:S(2)}) %copy-start.1) | copy-done | bytes 524312
  47.3 6.4 %shard_map.125 = (bf16[64,8192]{1,0:T(8,128)(2,1)}, bf16[32,128]{1,0:T(8,128)(2,1)}) custom-call(bf16[64,8192]{1,0:T(8,128)(2,1)} %bitcast.10, bf16[64,4096]{1,0:T(8,128)(2,1)} %get-tuple-element.12.own_ref, f32[16,128]{1,0:T(8,128)} %get-tuple-element.13.own_kept_ref, s32[32,128]{1,0:T(8,128)} %fusion.6.index_ref, bf16[64,4096]{1,0:T(8,128)(2,1)} %copy-done.1, ...), custom_call_target="tpu_custom_call" | custom-call | flops 1000000000 | bytes 4194304 | tf_op jit(solution)/shard_map/pallas_call | solution.py:428
  53.6 10.8 %shard_map.126 = bf16[16,32,128]{2,1,0:T(8,128)(2,1)} custom-call(bf16[32,128]{1,0:T(8,128)(2,1)} %get-tuple-element.16.value_ref), custom_call_target="tpu_custom_call" | custom-call | tf_op jit(solution)/shard_map/pallas_call | solution.py:335
  64.5 1.6 %convert_element_type.7.kept_ref = f32[16,32,128]{2,1,0:T(8,128)} convert(bf16[16,32,128]{2,1,0:T(8,128)(2,1)} %shard_map.126) | non-fusion elementwise | flops 65536 | bytes 393216 | tf_op jit(solution)/shard_map/convert_element_type | solution.py:493
  66.1 9.9 %shard_map.127 = bf16[64,8192]{1,0:T(8,128)(2,1)} custom-call(f32[16,32,128]{2,1,0:T(8,128)} %convert_element_type.7.kept_ref, s32[16,32,128]{2,1,0:T(8,128)} %get-tuple-element.17.index_ref, bf16[64,192]{1,0:T(8,128)(2,1)} %constant.52.clone.refs_3_.refs_4_.il, bf16[256,256]{1,0:T(8,128)(2,1)} %constant.53.clone.refs_4_.refs_5_.irh, ...), custom_call_target="tpu_custom_call" | custom-call | flops 1000000000 | bytes 4194304 | tf_op jit(solution)/shard_map/pallas_call | solution.py:428
Async XLA Ops:
  0.6 18.9 %copy-start = (bf16[128,4096]{1,0:T(8,128)(2,1)S(1)}, bf16[128,4096]{1,0:T(8,128)(2,1)}, u32[]{:S(2)}) copy-start(bf16[128,4096]{1,0:T(8,128)(2,1)} %g_ref.1) | copy-start | bytes 3145732
  23.0 4.6 %collective-permute-start = (bf16[384,128]{1,0:T(8,128)(2,1)S(1)}, bf16[384,128]{1,0:T(8,128)(2,1)S(1)}, u32[]{:S(2)}, u32[]{:S(2)}) collective-permute-start(bf16[384,128]{1,0:T(8,128)(2,1)S(1)} %get-tuple-element.18), channel_id=1, source_target_pairs={{0,16},{16,0},{1,17},{17,1},{2,18},{18,2},{3,19},{19,3},{4,20},{20... | collective-permute-start | bytes 294920 | tf_op jit(solution)/shard_map/ppermute | solution.py:461
  27.6 0.6 copy-start.2
  33.8 12.7 %collective-permute-start.1 = (bf16[64,4096]{1,0:T(8,128)(2,1)}, bf16[64,4096]{1,0:T(8,128)(2,1)S(1)}, u32[]{:S(2)}, u32[]{:S(2)}) collective-permute-start(bf16[64,4096]{1,0:T(8,128)(2,1)} %get-tuple-element.14), channel_id=1, source_target_pairs={{0,16},{16,0},{1,17},{17,1},{2,18},{18,2},{3,19},{19,3},{4,20},{20... | collective-permute-start | bytes 1572872 | tf_op jit(solution)/shard_map/ppermute | solution.py:471
  46.5 0.8 %copy-start.1 = (bf16[64,4096]{1,0:T(8,128)(2,1)}, bf16[64,4096]{1,0:T(8,128)(2,1)S(1)}, u32[]{:S(2)}) copy-start(bf16[64,4096]{1,0:T(8,128)(2,1)S(1)} %collective-permute-done.1.refs_0_) | copy-start | bytes 1572868

commit v4 on v3

--- a/solution.py
+++ b/solution.py
@@ -312,37 +312,47 @@
     return inner - 1 + count // inner - 1
 
 
-def gather_kernel(value_ref, out_ref, own_sem, send_sem, recv_sem):
-    me, _, near, far = neighbours(out_ref.shape[0])
-    section = lax.axis_index("section")
+def gather_kernel(value_ref, out_ref, held_ref, own_sem, send_sem, recv_sem):
+    count = out_ref.shape[0]
+    me, section = lax.axis_index("dp"), lax.axis_index("section")
+    peers = [lax.rem(me + k, count) for k in range(1, count)]
     barrier = pltpu.get_barrier_semaphore()
-    for peer in near + far:
+    for peer in peers:
         pl.semaphore_signal(barrier, inc=1, device_id=(section, peer), device_id_type=MESH)
-    own = pltpu.make_async_copy(value_ref, out_ref.at[me], own_sem)
+    own = pltpu.make_async_copy(value_ref, held_ref.at[me], own_sem)
     own.start()
-    pl.semaphore_wait(barrier, len(near) + len(far))
-    copies = gather_near(value_ref, out_ref, send_sem, recv_sem)
+    pl.semaphore_wait(barrier, count - 1)
+    copies = []
+    for k, peer in enumerate(peers):
+        copies.append(
+            pltpu.make_async_remote_copy(
+                src_ref=value_ref, dst_ref=held_ref.at[me],
+                send_sem=send_sem.at[k], recv_sem=recv_sem.at[k],
+                device_id=(section, peer), device_id_type=MESH,
+            )
+        )
+        copies[-1].start()
     own.wait()
     for copy in copies:
         copy.wait()
-    for copy in gather_far(out_ref, send_sem, recv_sem):
-        copy.wait()
+    out_ref[...] = held_ref[...].astype(F32)
 
 
 def gather(value, collective_id):
     count = lax.axis_size("dp")
     dma = pltpu.SemaphoreType.DMA
+    shape = (count,) + value.shape
     return pl.pallas_call(
         gather_kernel,
-        out_shape=jax.ShapeDtypeStruct((count,) + value.shape, value.dtype),
+        out_shape=jax.ShapeDtypeStruct(shape, F32),
         in_specs=[VMEM],
         out_specs=VMEM,
-        scratch_shapes=[dma] + [dma((gather_count(count),))] * 2,
+        scratch_shapes=[pltpu.VMEM(shape, value.dtype), dma] + [dma((count - 1,))] * 2,
         compiler_params=pltpu.CompilerParams(collective_id=collective_id, has_side_effects=True),
     )(value)
 
 
-CHUNKS = 2
+CHUNKS = 4
 
 
 def window_kernel(sections, weight_ref, index_ref, out_ref, index_out, local_sem, own_sem, send_sem, recv_sem,
@@ -490,7 +500,7 @@
         momentum[0, 0], own_out, own_kept, index, *received, *every,
         scratch=[pltpu.VMEM((tiles, per * kept_count), F32)],
     )
-    kept_all = gather(kept, 1).astype(F32)
+    kept_all = gather(kept, 1)
     update = call(
         decode_kernel,
         jax.ShapeDtypeStruct((rows, width), BF16),

time: 76.4 us -> 72.8 us (0.953)
  Pallas kernels: 55.8 us -> 53.8 us
  other arithmetic: 2.31 us -> 0.68 us
    pallas_call x1, Pallas kernels: 10.8 us -> 8.79 us  [gather(): pl.pallas_call(gather_kernel, out_shape=jax.ShapeDtypeStruct(shape, F32),...]
    convert_element_type x1 -> x0, other arithmetic: 1.63 us -> none  [local(): kept_all = gather(kept, 1).astype(F32)]
where the time goes in v4:
time: 72.8 us; the launch traced here: 72.5 us
  Pallas kernels  53.8 us (74%)
  waiting for transfers between devices  9.12 us (13%)
  matrix products  3.51 us (5%)
  local copies, waits for them, and re-layouts  2.4 us (3%)
  starting transfers between devices  2.24 us (3%)
    pallas_call x4, Pallas kernels, call(): pl.pallas_call(kernel, out_shape=out_shape, in_specs=[VMEM] * len(args),...  27.8 us
    pallas_call x1, Pallas kernels, windows(): pl.pallas_call(functools.partial(window_kernel, sections), out_shape=(jax...  17.3 us
    pallas_call x1, Pallas kernels, gather(): pl.pallas_call(gather_kernel, out_shape=jax.ShapeDtypeStruct(shape, F32),...  8.79 us
    ppermute x1, waiting for transfers between devices, local(): lax.ppermute(grads[step], 'section', pairs)  5.57 us
    ppermute x1, waiting for transfers between devices, local(): lax.ppermute(rounded, 'section', pairs)  3.55 us
    dot_general x1, matrix products, local(): sums = lax.dot_general(stack, window, NT, preferred_element_type=F32)  3.51 us
    unnamed x7, local copies, waits for them, and re-layouts  2.32 us
  transfers between devices with their start and end apart: 2, of which 2 were waited for; matrix products, arithmetic and copies ran while one was open for 0% of the time, Pallas kernels for 8%

profile of v4, /device:TPU:0, one launch (start us, length us, event | category | flops | bytes accessed | tf_op | source)
XLA Modules:
  0.0 72.5 jit_solution(9465415174821729395)
XLA Ops:
  0.6 0.0 copy-start
  0.7 0.9 %copy.14 = s32[1,1,128,32]{3,2,1,0:T(8,128)S(1)} copy(s32[1,1,128,32]{2,3,1,0:T(8,128)} %param.15) | data formatting | bytes 32768 | tf_op args[4]
  1.6 0.1 reshape_squeeze.3
  1.6 0.7 fusion.6.index_ref
  2.3 17.3 %shard_map.122 = (bf16[2,64,4096]{2,1,0:T(8,128)(2,1)}, s32[16,32,128]{2,1,0:T(8,128)}) custom-call(bf16[64,8192]{1,0:T(8,128)(2,1)} %bitcast.8, s32[32,128]{1,0:T(8,128)} %fusion.6.index_ref), custom_call_target="tpu_custom_call" | custom-call | tf_op jit(solution)/shard_map/pallas_call | solution.py:424
  19.6 0.0 copy-done
  19.6 3.5 %fusion.8 = (bf16[384,128]{1,0:T(8,128)(2,1)S(1)}, f32[384,128]{1,0:T(8,128)}) fusion(bf16[128,4096]{1,0:T(8,128)(2,1)} %bitcast.11, bf16[128,4096]{1,0:T(8,128)(2,1)S(1)} %copy-done, bf16[128,4096]{1,0:T(8,128)(2,1)} %x_ref.1), kind=kOutput, calls=%fused_computation.10 | convolution fusion | flops 412139520 | bytes 3440640 | tf_op jit(solution)/shard_map/dot_general | solution.py:469
  23.1 1.1 %collective-permute-start = (bf16[384,128]{1,0:T(8,128)(2,1)S(1)}, bf16[384,128]{1,0:T(8,128)(2,1)S(1)}, u32[]{:S(2)}, u32[]{:S(2)}) collective-permute-start(bf16[384,128]{1,0:T(8,128)(2,1)S(1)} %get-tuple-element.18), channel_id=1, source_target_pairs={{0,16},{16,0},{1,17},{17,1},{2,18},{18,2},{3,19},{19,3},{4,20},{20... | collective-permute-start | bytes 294920 | tf_op jit(solution)/shard_map/ppermute | solution.py:471
  24.2 3.5 %collective-permute-done.got_ref = bf16[384,128]{1,0:T(8,128)(2,1)S(1)} collective-permute-done((bf16[384,128]{1,0:T(8,128)(2,1)S(1)}, bf16[384,128]{1,0:T(8,128)(2,1)S(1)}, u32[]{:S(2)}, u32[]{:S(2)}) %collective-permute-start) | collective-permute-done | bytes 98336 | tf_op jit(solution)/shard_map/ppermute | solution.py:471
  27.7 0.0 copy-start.2
  27.7 0.6 copy-done.2
  28.4 5.5 %shard_map.123 = (bf16[64,4096]{1,0:T(8,128)(2,1)}, bf16[64,4096]{1,0:T(8,128)(2,1)}) custom-call(f32[384,128]{1,0:T(8,128)} %get-tuple-element.19.sums_ref, bf16[384,128]{1,0:T(8,128)(2,1)} %copy-done.2, bf16[128,4096]{1,0:T(8,128)(2,1)} %x_ref.1, bf16[128,4096]{1,0:T(8,128)(2,1)} %g_ref.1, bf16[128,4096]{1,0:T(8,128)(2,1)} %bitcast.12), custom_call_target="tpu_custom_call" | custom-call | flops 1000000000 | bytes 4194304 | tf_op jit(solution)/shard_map/pallas_call | solution.py:438
  33.9 1.2 %collective-permute-start.1 = (bf16[64,4096]{1,0:T(8,128)(2,1)}, bf16[64,4096]{1,0:T(8,128)(2,1)S(1)}, u32[]{:S(2)}, u32[]{:S(2)}) collective-permute-start(bf16[64,4096]{1,0:T(8,128)(2,1)} %get-tuple-element.14), channel_id=1, source_target_pairs={{0,16},{16,0},{1,17},{17,1},{2,18},{18,2},{3,19},{19,3},{4,20},{20... | collective-permute-start | bytes 1572872 | tf_op jit(solution)/shard_map/ppermute | solution.py:481
  35.1 5.9 %shard_map.124 = (bf16[64,4096]{1,0:T(8,128)(2,1)}, f32[16,128]{1,0:T(8,128)}) custom-call(bf16[64,8192]{1,0:T(8,128)(2,1)} %bitcast.9, bf16[64,4096]{1,0:T(8,128)(2,1)} %get-tuple-element.11.grad_ref, s32[32,128]{1,0:T(8,128)} %fusion.6.index_ref, bf16[64,192]{1,0:T(8,128)(2,1)} %constant.55.clone.refs_0_.refs_1_, ...), custom_call_target="tpu_custom_call" | custom-call | flops 1000000000 | bytes 4194304 | tf_op jit(solution)/shard_map/pallas_call | solution.py:438
  41.0 5.6 %collective-permute-done.1.refs_0_ = bf16[64,4096]{1,0:T(8,128)(2,1)S(1)} collective-permute-done((bf16[64,4096]{1,0:T(8,128)(2,1)}, bf16[64,4096]{1,0:T(8,128)(2,1)S(1)}, u32[]{:S(2)}, u32[]{:S(2)}) %collective-permute-start.1) | collective-permute-done | bytes 524320 | tf_op jit(solution)/shard_map/ppermute | solution.py:481
  46.5 0.0 copy-start.1
  46.5 0.8 %copy-done.1 = bf16[64,4096]{1,0:T(8,128)(2,1)} copy-done((bf16[64,4096]{1,0:T(8,128)(2,1)}, bf16[64,4096]{1,0:T(8,128)(2,1)S(1)}, u32[]{:S(2)}) %copy-start.1) | copy-done | bytes 524312
  47.3 6.4 %shard_map.125 = (bf16[64,8192]{1,0:T(8,128)(2,1)}, bf16[32,128]{1,0:T(8,128)(2,1)}) custom-call(bf16[64,8192]{1,0:T(8,128)(2,1)} %bitcast.10, bf16[64,4096]{1,0:T(8,128)(2,1)} %get-tuple-element.12.own_ref, f32[16,128]{1,0:T(8,128)} %get-tuple-element.13.own_kept_ref, s32[32,128]{1,0:T(8,128)} %fusion.6.index_ref, bf16[64,4096]{1,0:T(8,128)(2,1)} %copy-done.1, ...), custom_call_target="tpu_custom_call" | custom-call | flops 1000000000 | bytes 4194304 | tf_op jit(solution)/shard_map/pallas_call | solution.py:438
  53.7 8.8 %shard_map.126.kept_ref = f32[16,32,128]{2,1,0:T(8,128)} custom-call(bf16[32,128]{1,0:T(8,128)(2,1)} %get-tuple-element.16.value_ref), custom_call_target="tpu_custom_call" | custom-call | tf_op jit(solution)/shard_map/pallas_call | solution.py:345
  62.5 10.0 %shard_map.127 = bf16[64,8192]{1,0:T(8,128)(2,1)} custom-call(f32[16,32,128]{2,1,0:T(8,128)} %shard_map.126.kept_ref, s32[16,32,128]{2,1,0:T(8,128)} %get-tuple-element.17.index_ref, bf16[64,192]{1,0:T(8,128)(2,1)} %constant.52.clone.refs_3_.refs_4_.il, bf16[256,256]{1,0:T(8,128)(2,1)} %constant.53.clone.refs_4_.refs_5_.irh, ...), custom_call_target="tpu_custom_call" | custom-call | flops 1000000000 | bytes 4194304 | tf_op jit(solution)/shard_map/pallas_call | solution.py:438
Async XLA Ops:
  0.6 19.0 %copy-start = (bf16[128,4096]{1,0:T(8,128)(2,1)S(1)}, bf16[128,4096]{1,0:T(8,128)(2,1)}, u32[]{:S(2)}) copy-start(bf16[128,4096]{1,0:T(8,128)(2,1)} %g_ref.1) | copy-start | bytes 3145732
  23.1 4.6 %collective-permute-start = (bf16[384,128]{1,0:T(8,128)(2,1)S(1)}, bf16[384,128]{1,0:T(8,128)(2,1)S(1)}, u32[]{:S(2)}, u32[]{:S(2)}) collective-permute-start(bf16[384,128]{1,0:T(8,128)(2,1)S(1)} %get-tuple-element.18), channel_id=1, source_target_pairs={{0,16},{16,0},{1,17},{17,1},{2,18},{18,2},{3,19},{19,3},{4,20},{20... | collective-permute-start | bytes 294920 | tf_op jit(solution)/shard_map/ppermute | solution.py:471
  27.7 0.6 copy-start.2
  33.9 12.7 %collective-permute-start.1 = (bf16[64,4096]{1,0:T(8,128)(2,1)}, bf16[64,4096]{1,0:T(8,128)(2,1)S(1)}, u32[]{:S(2)}, u32[]{:S(2)}) collective-permute-start(bf16[64,4096]{1,0:T(8,128)(2,1)} %get-tuple-element.14), channel_id=1, source_target_pairs={{0,16},{16,0},{1,17},{17,1},{2,18},{18,2},{3,19},{19,3},{4,20},{20... | collective-permute-start | bytes 1572872 | tf_op jit(solution)/shard_map/ppermute | solution.py:481
  46.5 0.8 %copy-start.1 = (bf16[64,4096]{1,0:T(8,128)(2,1)}, bf16[64,4096]{1,0:T(8,128)(2,1)S(1)}, u32[]{:S(2)}) copy-start(bf16[64,4096]{1,0:T(8,128)(2,1)S(1)} %collective-permute-done.1.refs_0_) | copy-start | bytes 1572868
